TPU v7x, 512 devices: a whole 4x8x8 slice. The times are simulated.
512 devices in a mesh: rows: 512 (over z, y, x, core).
Axes of the slice: x: 4, y: 8, z: 8, core: 2. Of those that a mesh axis runs over, the one named last changes fastest.
Arguments:
- adj_diag: int32 [8192, 512], P('rows'), may hold values from -2147483648 to 2147483647
- adj_right: int32 [8192, 512], P('rows'), may hold values from -2147483648 to 2147483647
- alive_diag: int32 [8192, 512], P('rows'), may hold values from -2147483648 to 2147483647
- alive_right: int32 [8192, 512], P('rows'), may hold values from -2147483648 to 2147483647
- truss_k: int32 [1], replicated, may hold values from 130 to 193
Outputs:
- support_field: float32 [262144, 1024], P('rows')
- removed_counts: int32 [3], replicated
All inputs are finite; a program needn't handle non-finite values.
Results may differ from a plain program's by a relative error of at most 0.0003.
Values may be sent and summed in bfloat16 or wider, within the bound.
No kernel may reach another device: no remote copies, remote signals or barrier semaphores. Data moves between devices by JAX's collectives and lax.ppermute only.
A program may use at most 64 MiB of HBM per device.

v0:
```python
import jax
import jax.numpy as jnp
from jax import lax
from jax.sharding import Mesh
from jax.sharding import PartitionSpec as P

ITERS = 3
ROWS = ("rows_0", "rows_1", "rows_2", "rows_3")


def shifted(array, axis, by):
    count = lax.axis_size(axis)
    return lax.ppermute(array, axis, [(i, (i + by) % count) for i in range(count)])


def over_axes(array, axes):
    for axis in axes:
        array = lax.psum(array, axis)
    return array


def unpack_tile(packed):
    shifts = jnp.arange(32, dtype=jnp.int32)
    tile_bits = packed[:, None, :] >> shifts[None, :, None] & 1
    return tile_bits.reshape(packed.shape[0] * 32, packed.shape[1])


def pack_bits(tile_bits):
    shifts = jnp.arange(32, dtype=jnp.int32)
    sectioned = tile_bits.reshape(tile_bits.shape[0] // 32, 32, tile_bits.shape[1])
    return jnp.sum(sectioned << shifts[None, :, None], axis=1, dtype=jnp.int32)


def within_tile(packed):
    upper_half = jnp.triu(unpack_tile(packed), 1)
    return (upper_half + upper_half.T).astype(jnp.bfloat16)


def across_tile(packed):
    return unpack_tile(packed).astype(jnp.bfloat16)


def pack_across(across):
    return pack_bits(across.astype(jnp.int32))


def fold_within(within):
    width = within.shape[0]
    half = width // 2
    row_ids = lax.broadcasted_iota(jnp.int32, (half, width), 0)
    col_ids = lax.broadcasted_iota(jnp.int32, (half, width), 1)
    flipped = within[half:][::-1, ::-1]
    folded = jnp.where(col_ids > row_ids, within[:half], flipped)
    return pack_bits(folded.astype(jnp.int32))


def unfold_within(packed):
    folded = unpack_tile(packed)
    half = folded.shape[0]
    width = folded.shape[1]
    row_ids = lax.broadcasted_iota(jnp.int32, (half, width), 0)
    col_ids = lax.broadcasted_iota(jnp.int32, (half, width), 1)
    top_rows = jnp.where(col_ids > row_ids, folded, jnp.zeros_like(folded))
    bottom_rows = jnp.where(col_ids < row_ids, folded, jnp.zeros_like(folded))[::-1, ::-1]
    upper_half = jnp.concatenate([top_rows, bottom_rows], axis=0)
    return (upper_half + upper_half.T).astype(jnp.bfloat16)


def support_within(prev_across, within, across):
    inside = lax.dot_general(
        prev_across, prev_across, (((0,), (0,)), ((), ())), preferred_element_type=jnp.float32
    )
    inside = inside + jnp.dot(within, within, preferred_element_type=jnp.float32)
    return inside + lax.dot_general(
        across, across, (((1,), (1,)), ((), ())), preferred_element_type=jnp.float32
    )


def support_across(within, across, next_within):
    between = jnp.dot(within, across, preferred_element_type=jnp.float32)
    return between + jnp.dot(across, next_within, preferred_element_type=jnp.float32)


def keep_edges(support, tile_mask, thresh):
    return jnp.where(support >= thresh, tile_mask, jnp.zeros_like(tile_mask))


def peel(prev_across, within, across, next_within, thresh):
    inside = support_within(prev_across, within, across)
    between = support_across(within, across, next_within)
    return (
        inside,
        between,
        keep_edges(inside, within, thresh),
        keep_edges(between, across, thresh),
    )


def tally(within, new_within, across, new_across):
    removed = jnp.sum((within - new_within).astype(jnp.int32)) // 2
    removed = removed + jnp.sum((across - new_across).astype(jnp.int32))
    return removed


def on_device(adj_diag, adj_right, alive_diag, alive_right, truss_k):
    within = within_tile(adj_diag & alive_diag)
    across_words = adj_right & alive_right
    across = across_tile(across_words)
    thresh = (truss_k[0] - 2).astype(jnp.float32)
    counts = []
    for step in range(ITERS):
        prev_across = across_tile(shifted(pack_across(across), ROWS, 1))
        next_within = unfold_within(shifted(fold_within(within), ROWS, -1))
        inside, between, new_within, new_across = peel(
            prev_across, within, across, next_within, thresh
        )
        counts.append(tally(within, new_within, across, new_across))
        within, across = (new_within, new_across)
    stacked = jnp.stack(counts)
    stacked = over_axes(stacked, ROWS)
    support = jnp.concatenate(
        [inside * within.astype(jnp.float32), between * across.astype(jnp.float32)], axis=1
    )
    return (support, stacked)


def solution(mesh):
    split = Mesh(mesh.devices.reshape(8, 8, 4, 2), ("rows_0", "rows_1", "rows_2", "rows_3"))
    placed = (P(ROWS, None), P(ROWS, None), P(ROWS, None), P(ROWS, None), P())
    return jax.shard_map(
        on_device, mesh=split, in_specs=placed, out_specs=(P(ROWS, None), P()), check_vma=False
    )
```

profile of v0, /device:TPU:1, one launch (start us, length us, event | category | flops | bytes accessed | tf_op | source)
XLA Modules:
  0.0 128.3 jit_solution(3447967203919431901)
XLA Ops:
  0.7 0.8 and.74
  1.5 0.2 fusion.17
  1.7 0.3 copy.7
  2.1 0.3 fusion.14
  2.4 0.9 rev.18
  3.5 8.7 %collective-permute-start.1 = (s32[8,512]{1,0:T(8,128)S(1)}, s32[8,512]{1,0:T(8,128)S(1)}, u32[]{:S(2)}, u32[]{:S(2)}) collective-permute-start(s32[8,512]{1,0:T(8,128)S(1)} %fusion.25), channel_id=1, source_target_pairs={{0,511},{1,0},{2,1},{3,2},{4,3},{5,4},{6,5},{7,6},{8,7},{9,8},{10,... | collective-permute-start | bytes 49160 | tf_op jit(solution)/shard_map/ppermute | solution.py:13
  12.2 0.4 and_convert_fusion.3
  12.6 1.9 %collective-permute-start = (s32[16,512]{1,0:T(8,128)S(1)}, s32[16,512]{1,0:T(8,128)S(1)}, u32[]{:S(2)}, u32[]{:S(2)}) collective-permute-start(s32[16,512]{1,0:T(8,128)S(1)} %get-tuple-element.9), channel_id=1, source_target_pairs={{0,1},{1,2},{2,3},{3,4},{4,5},{5,6},{6,7},{7,8},{8,9},{9,10},{10,1... | collective-permute-start | bytes 98312 | tf_op jit(solution)/shard_map/ppermute | solution.py:13
  14.6 1.4 %fusion.47 = f32[512,512]{1,0:T(8,128)} fusion(bf16[512,512]{1,0:T(8,128)(2,1)S(1)} %get-tuple-element.17, bf16[512,512]{1,0:T(8,128)(2,1)S(1)} %get-tuple-element.16), kind=kOutput, calls=%fused_computation.93 | convolution fusion | flops 268435456 | bytes 2097152 | tf_op jit(solution)/shard_map/dot_general | solution.py:80
  16.9 0.8 rev.19
  17.6 1.1 pad_add_fusion
  18.7 2.6 %copy.8 = s32[512,512]{0,1:T(8,128)} copy(s32[512,512]{1,0:T(8,128)} %pad_add_fusion) | data formatting | bytes 2097152 | tf_op jit(solution)/shard_map/concatenate | solution.py:65
  21.3 2.2 %fusion.8 = (s32[16,512]{1,0:T(8,128)S(1)}, bf16[512,512]{1,0:T(8,128)(2,1)S(1)}) fusion(bf16[512,512]{1,0:T(8,128)(2,1)S(1)} %get-tuple-element.16, f32[]{:T(128)} %bitcast.4, f32[512,512]{1,0:T(8,128)} %fusion.47, s32[512,512]{0,1:T(8,128)} %copy.8, s32[256,512]{1,0:T(8,128)S(1)} %rev.19, s32[256,512]{1,0:T(8,128)S(1)} %get-tuple-element.14), kind=kOutput, calls=%fused_computation.25 | convolution fusion | flops 270786560 | bytes 4227076 | tf_op jit(solution)/shard_map/dot_general | solution.py:81
  23.5 1.9 %collective-permute-start.4 = (s32[16,512]{1,0:T(8,128)S(1)}, s32[16,512]{1,0:T(8,128)S(1)}, u32[]{:S(2)}, u32[]{:S(2)}) collective-permute-start(s32[16,512]{1,0:T(8,128)S(1)} %get-tuple-element.20), channel_id=1, source_target_pairs={{0,1},{1,2},{2,3},{3,4},{4,5},{5,6},{6,7},{7,8},{8,9},{9,10},{10,1... | collective-permute-start | bytes 98312 | tf_op jit(solution)/shard_map/ppermute | solution.py:13
  25.5 0.5 convolution_bitcast_fusion.2
  26.0 0.4 convolution_add_fusion.8
  26.4 0.5 fusion.7
  26.9 0.9 rev.20
  28.0 10.1 %collective-permute-start.2 = (s32[8,512]{1,0:T(8,128)S(1)}, s32[8,512]{1,0:T(8,128)S(1)}, u32[]{:S(2)}, u32[]{:S(2)}) collective-permute-start(s32[8,512]{1,0:T(8,128)S(1)} %fusion.24), channel_id=1, source_target_pairs={{0,511},{1,0},{2,1},{3,2},{4,3},{5,4},{6,5},{7,6},{8,7},{9,8},{10,... | collective-permute-start | bytes 49160 | tf_op jit(solution)/shard_map/ppermute | solution.py:13
  38.1 0.5 convolution_bitcast_fusion
  38.6 0.4 convolution_add_fusion.4
  39.1 0.5 fusion.6
  39.6 0.9 rev.22
  40.6 9.1 %collective-permute-start.5 = (s32[8,512]{1,0:T(8,128)S(1)}, s32[8,512]{1,0:T(8,128)S(1)}, u32[]{:S(2)}, u32[]{:S(2)}) collective-permute-start(s32[8,512]{1,0:T(8,128)S(1)} %fusion.23), channel_id=1, source_target_pairs={{0,511},{1,0},{2,1},{3,2},{4,3},{5,4},{6,5},{7,6},{8,7},{9,8},{10,... | collective-permute-start | bytes 49160 | tf_op jit(solution)/shard_map/ppermute | solution.py:13
  49.7 1.4 %fusion.48 = f32[512,512]{1,0:T(8,128)} fusion(bf16[512,512]{1,0:T(8,128)(2,1)S(1)} %fusion.7, bf16[512,512]{1,0:T(8,128)(2,1)S(1)} %get-tuple-element.21), kind=kOutput, calls=%fused_computation.94 | convolution fusion | flops 268435456 | bytes 2097152 | tf_op jit(solution)/shard_map/dot_general | solution.py:80
  51.1 1.4 %fusion.28 = (s32[256,512]{1,0:T(8,128)}, s32[256,512]{1,0:T(8,128)}, s32[256,512]{1,0:T(8,128)}, s32[256,512]{1,0:T(8,128)S(1)}) fusion(s32[8,512]{1,0:T(8,128)S(1)} %collective-permute-done.5, s32[256]{0:T(256)S(1)} %shift_left.64, s32[8,512]{1,0:T(8,128)S(1)} %collective-permute-done.2), kind=kLoop, calls=%fused_computation.69 | loop fusion | flops 1310720 | bytes 2130944 | tf_op jit(solution)/shard_map/jit(_where)/select_n | solution.py:63
  52.5 3.9 %rev.21 = s32[256,512]{1,0:T(8,128)S(1)} reverse(s32[256,512]{1,0:T(8,128)} %get-tuple-element.18), dimensions={0,1} | reverse | bytes 1048576 | tf_op jit(solution)/shard_map/rev | solution.py:64
  56.4 1.1 pad_add_fusion.1
  57.5 2.6 %copy.9 = s32[512,512]{0,1:T(8,128)} copy(s32[512,512]{1,0:T(8,128)} %pad_add_fusion.1) | data formatting | bytes 2097152 | tf_op jit(solution)/shard_map/concatenate | solution.py:65
  60.1 2.4 %fusion.9 = (s32[16,512]{1,0:T(8,128)S(1)}, bf16[512,512]{1,0:T(8,128)(2,1)S(1)}) fusion(bf16[512,512]{1,0:T(8,128)(2,1)S(1)} %get-tuple-element.21, f32[]{:T(128)} %bitcast.4, f32[512,512]{1,0:T(8,128)} %fusion.48, s32[512,512]{0,1:T(8,128)} %copy.9, s32[256,512]{1,0:T(8,128)S(1)} %rev.21, s32[256,512]{1,0:T(8,128)} %copy-done.1), kind=kOutput, calls=%fused_computation.27 | convolution fusion | flops 270786560 | bytes 4227076 | tf_op jit(solution)/shard_map/dot_general | solution.py:81
  62.5 1.9 %collective-permute-start.3 = (s32[16,512]{1,0:T(8,128)S(1)}, s32[16,512]{1,0:T(8,128)S(1)}, u32[]{:S(2)}, u32[]{:S(2)}) collective-permute-start(s32[16,512]{1,0:T(8,128)S(1)} %get-tuple-element.24), channel_id=1, source_target_pairs={{0,1},{1,2},{2,3},{3,4},{4,5},{5,6},{6,7},{7,8},{8,9},{9,10},{10,1... | collective-permute-start | bytes 98312 | tf_op jit(solution)/shard_map/ppermute | solution.py:13
  64.4 3.8 %rev.23 = s32[256,512]{1,0:T(8,128)S(1)} reverse(s32[256,512]{1,0:T(8,128)} %get-tuple-element.11), dimensions={0,1} | reverse | bytes 1048576 | tf_op jit(solution)/shard_map/rev | solution.py:64
  68.2 2.1 %pad_add_fusion.2 = s32[512,512]{1,0:T(8,128)} fusion(s32[256,512]{1,0:T(8,128)S(1)} %rev.23, s32[256,512]{1,0:T(8,128)} %get-tuple-element.10), kind=kLoop, calls=%fused_computation.23 | loop fusion | flops 262144 | bytes 2097152 | tf_op jit(solution)/shard_map/concatenate | solution.py:65
  70.3 2.5 %copy.13 = s32[512,512]{0,1:T(8,128)} copy(s32[512,512]{1,0:T(8,128)} %pad_add_fusion.2) | data formatting | bytes 2097152 | tf_op jit(solution)/shard_map/concatenate | solution.py:65
  72.8 0.4 fusion.49
  73.3 0.6 copy-done
  73.9 0.3 copy-done.3
  74.2 1.5 %convert_multiply_fusion = (f32[512,512]{1,0:T(8,128)}, f32[512,512]{1,0:T(8,128)S(1)}) fusion(bf16[512,512]{1,0:T(8,128)(2,1)S(1)} %get-tuple-element.25, f32[]{:T(128)} %bitcast.4, f32[512,512]{1,0:T(8,128)S(1)} %fusion.49, s32[512,512]{0,1:T(8,128)S(1)} %copy-done.3, s32[256,512]{1,0:T(8,128)S(1)} %rev.23, s32[256,512]{1,0:T(8,128)S(1)} %copy-done), kind=kOutput, calls=%fused_computation.48 | convolution fusion | flops 270532608 | bytes 5767172 | tf_op jit(solution)/shard_map/dot_general | solution.py:81
  75.7 1.5 %convert_reduce_fusion.4 = (s32[]{:T(128)}, s32[]{:T(128)}, s32[]{:T(128)}) fusion(bf16[512,512]{1,0:T(8,128)(2,1)S(1)} %get-tuple-element.21, s32[512]{0:T(512)S(1)} %shift_right_arithmetic.162, s32[16,512]{1,0:T(8,128)S(1)} %and.71, bf16[512,512]{1,0:T(8,128)(2,1)S(1)} %get-tuple-element.25, f32[512,512]{1,0:T(8,128)S(1)} %get-tuple-element.23, f32[]{:T(128)} %bitcast.4), kind=kLoop, calls=%fused_computation.46 | loop fusion | flops 4718589 | bytes 2131984 | tf_op jit(solution)/shard_map/reduce_sum | solution.py:101
  77.2 0.5 convolution_bitcast_fusion.1
  77.7 0.4 convolution_add_fusion.2
  78.1 1.5 %convert_multiply_fusion.1 = (f32[512,512]{1,0:T(8,128)}, f32[512,512]{1,0:T(8,128)S(1)}) fusion(bf16[512,512]{1,0:T(8,128)(2,1)S(1)} %fusion.6, f32[]{:T(128)} %bitcast.4, f32[512,512]{1,0:T(8,128)S(1)} %convolution_add_fusion.2, bf16[512,512]{1,0:T(8,128)(2,1)S(1)} %get-tuple-element.25), kind=kOutput, calls=%fused_computation.49 | convolution fusion | flops 269746176 | bytes 4194308 | tf_op jit(solution)/shard_map/dot_general | solution.py:74
  79.6 1.4 %convert_reduce_fusion.5 = (s32[]{:T(128)}, s32[]{:T(128)}, s32[]{:T(128)}) fusion(bf16[512,512]{1,0:T(8,128)(2,1)S(1)} %get-tuple-element.17, bf16[512,512]{1,0:T(8,128)(2,1)S(1)} %fusion.7, bf16[512,512]{1,0:T(8,128)(2,1)S(1)} %fusion.6, f32[512,512]{1,0:T(8,128)S(1)} %get-tuple-element.27, f32[]{:T(128)} %bitcast.4), kind=kLoop, calls=%fused_computation.47 | loop fusion | flops 2883581 | bytes 2621456 | tf_op jit(solution)/shard_map/reduce_sum | solution.py:100
  90.5 7.0 %psum.28 = s32[3]{0:T(128)S(1)} all-reduce(s32[3]{0:T(128)S(1)} %pad_add_fusion.3), channel_id=1, replica_groups=mesh['rows_0'=8,'rows_1'=8,'rows_2'=4,'rows_3'=2] {'rows_0'}, use_global_device_ids=true, to_apply=%region_12.13 | all-reduce | flops 3 | bytes 24 | tf_op jit(solution)/shard_map/psum | solution.py:18
  97.5 7.0 %psum.29 = s32[3]{0:T(128)S(1)} all-reduce(s32[3]{0:T(128)S(1)} %psum.28), channel_id=1, replica_groups=mesh['rows_0'=8,'rows_1'=8,'rows_2'=4,'rows_3'=2] {'rows_1'}, use_global_device_ids=true, to_apply=%region_13.14 | all-reduce | flops 3 | bytes 24 | tf_op jit(solution)/shard_map/psum | solution.py:18
  104.5 11.6 %psum.30 = s32[3]{0:T(128)S(1)} all-reduce(s32[3]{0:T(128)S(1)} %psum.29), channel_id=1, replica_groups=mesh['rows_0'=8,'rows_1'=8,'rows_2'=4,'rows_3'=2] {'rows_2'}, use_global_device_ids=true, to_apply=%region_14.15 | all-reduce | flops 3 | bytes 24 | tf_op jit(solution)/shard_map/psum | solution.py:18
  116.1 9.4 %psum.31 = s32[3]{0:T(128)} all-reduce(s32[3]{0:T(128)S(1)} %psum.30), channel_id=1, replica_groups=mesh['rows_0'=8,'rows_1'=8,'rows_2'=4,'rows_3'=2] {'rows_3'}, use_global_device_ids=true, to_apply=%region_15.16 | all-reduce | flops 3 | bytes 24 | tf_op jit(solution)/shard_map/psum | solution.py:18
  125.5 2.8 %pad_maximum_fusion = f32[512,1024]{1,0:T(8,128)} fusion(f32[512,512]{1,0:T(8,128)} %get-tuple-element.22, f32[512,512]{1,0:T(8,128)S(1)} %copy-done.2), kind=kLoop, calls=%fused_computation | loop fusion | flops 524288 | bytes 4194304 | tf_op jit(solution)/shard_map/concatenate | solution.py:121
  (29 shorter events, 0.9 us)
Async XLA Ops:
  0.6 1.4 %copy-start.4 = (s32[16,512]{1,0:T(8,128)S(1)}, s32[16,512]{1,0:T(8,128)}, u32[]{:S(2)}) copy-start(s32[16,512]{1,0:T(8,128)} %param.6) | copy-start | bytes 98308
  0.6 1.4 %copy-start.5 = (s32[16,512]{1,0:T(8,128)S(1)}, s32[16,512]{1,0:T(8,128)}, u32[]{:S(2)}) copy-start(s32[16,512]{1,0:T(8,128)} %param.8) | copy-start | bytes 98308
  3.5 13.2 %collective-permute-start.1 = (s32[8,512]{1,0:T(8,128)S(1)}, s32[8,512]{1,0:T(8,128)S(1)}, u32[]{:S(2)}, u32[]{:S(2)}) collective-permute-start(s32[8,512]{1,0:T(8,128)S(1)} %fusion.25), channel_id=1, source_target_pairs={{0,511},{1,0},{2,1},{3,2},{4,3},{5,4},{6,5},{7,6},{8,7},{9,8},{10,... | collective-permute-start | bytes 49160 | tf_op jit(solution)/shard_map/ppermute | solution.py:13
  12.6 12.8 %collective-permute-start = (s32[16,512]{1,0:T(8,128)S(1)}, s32[16,512]{1,0:T(8,128)S(1)}, u32[]{:S(2)}, u32[]{:S(2)}) collective-permute-start(s32[16,512]{1,0:T(8,128)S(1)} %get-tuple-element.9), channel_id=1, source_target_pairs={{0,1},{1,2},{2,3},{3,4},{4,5},{5,6},{6,7},{7,8},{8,9},{9,10},{10,1... | collective-permute-start | bytes 98312 | tf_op jit(solution)/shard_map/ppermute | solution.py:13
  23.5 14.6 %collective-permute-start.4 = (s32[16,512]{1,0:T(8,128)S(1)}, s32[16,512]{1,0:T(8,128)S(1)}, u32[]{:S(2)}, u32[]{:S(2)}) collective-permute-start(s32[16,512]{1,0:T(8,128)S(1)} %get-tuple-element.20), channel_id=1, source_target_pairs={{0,1},{1,2},{2,3},{3,4},{4,5},{5,6},{6,7},{7,8},{8,9},{9,10},{10,1... | collective-permute-start | bytes 98312 | tf_op jit(solution)/shard_map/ppermute | solution.py:13
  28.0 23.1 %collective-permute-start.2 = (s32[8,512]{1,0:T(8,128)S(1)}, s32[8,512]{1,0:T(8,128)S(1)}, u32[]{:S(2)}, u32[]{:S(2)}) collective-permute-start(s32[8,512]{1,0:T(8,128)S(1)} %fusion.24), channel_id=1, source_target_pairs={{0,511},{1,0},{2,1},{3,2},{4,3},{5,4},{6,5},{7,6},{8,7},{9,8},{10,... | collective-permute-start | bytes 49160 | tf_op jit(solution)/shard_map/ppermute | solution.py:13
  40.6 10.5 %collective-permute-start.5 = (s32[8,512]{1,0:T(8,128)S(1)}, s32[8,512]{1,0:T(8,128)S(1)}, u32[]{:S(2)}, u32[]{:S(2)}) collective-permute-start(s32[8,512]{1,0:T(8,128)S(1)} %fusion.23), channel_id=1, source_target_pairs={{0,511},{1,0},{2,1},{3,2},{4,3},{5,4},{6,5},{7,6},{8,7},{9,8},{10,... | collective-permute-start | bytes 49160 | tf_op jit(solution)/shard_map/ppermute | solution.py:13
  52.5 5.0 %copy-start.1 = (s32[256,512]{1,0:T(8,128)}, s32[256,512]{1,0:T(8,128)S(1)}, u32[]{:S(2)}) copy-start(s32[256,512]{1,0:T(8,128)S(1)} %get-tuple-element.19) | copy-start | bytes 1572868
  62.5 14.7 %collective-permute-start.3 = (s32[16,512]{1,0:T(8,128)S(1)}, s32[16,512]{1,0:T(8,128)S(1)}, u32[]{:S(2)}, u32[]{:S(2)}) collective-permute-start(s32[16,512]{1,0:T(8,128)S(1)} %get-tuple-element.24), channel_id=1, source_target_pairs={{0,1},{1,2},{2,3},{3,4},{4,5},{5,6},{6,7},{7,8},{8,9},{9,10},{10,1... | collective-permute-start | bytes 98312 | tf_op jit(solution)/shard_map/ppermute | solution.py:13
  72.8 1.0 copy-start
  72.8 1.4 %copy-start.3 = (s32[512,512]{0,1:T(8,128)S(1)}, s32[512,512]{0,1:T(8,128)}, u32[]{:S(2)}) copy-start(s32[512,512]{0,1:T(8,128)} %copy.13) | copy-start | bytes 3145732
  79.6 45.9 %copy-start.2 = (f32[512,512]{1,0:T(8,128)S(1)}, f32[512,512]{1,0:T(8,128)}, u32[]{:S(2)}) copy-start(f32[512,512]{1,0:T(8,128)} %get-tuple-element.26) | copy-start | bytes 3145732
where the time goes:
time: 129 us; the launch traced here: 128 us
  blocking collectives  35 us (27%)
  starting transfers between devices  33.7 us (26%)
  local copies, waits for them, and re-layouts  20.4 us (16%)
  matrix products  14.6 us (11%)
  other arithmetic  13.6 us (11%)
  between operations  11.1 us (9%)
    psum x4, blocking collectives, over_axes(): array = lax.psum(array, axis)  35 us
    ppermute x6, starting transfers between devices, shifted(): lax.ppermute(array, axis, [(i, (i + by) % count) for i in range(count)])  33.7 us
    rev x3, local copies, waits for them, and re-layouts, unfold_within(): jnp.where(col_ids < row_ids, folded, jnp.zeros_like(folded))[::-1, ::-1]  8.42 us
    concatenate x3, local copies, waits for them, and re-layouts, unfold_within(): upper_half = jnp.concatenate([top_rows, bottom_rows], axis=0)  7.69 us
    dot_general x3, matrix products, support_across(): jnp.dot(across, next_within, preferred_element_type=jnp.float32)  6.13 us
    concatenate x3, other arithmetic, unfold_within(): upper_half = jnp.concatenate([top_rows, bottom_rows], axis=0)  4.27 us
    dot_general x3, matrix products, support_across(): between = jnp.dot(within, across, preferred_element_type=jnp.float32)  3.25 us
    concatenate x1, other arithmetic, on_device(): jnp.concatenate([inside * within.astype(jnp.float32), between * across.as...  2.76 us
  transfers between devices with their start and end apart: 6, of which 0 were waited for; matrix products, arithmetic and copies ran while one was open for 21% of the time, Pallas kernels for 0%

commit v1 on v0

v1 whole, which is shorter than its diff:
```python
import jax
import jax.numpy as jnp
from jax import lax
from jax.experimental import pallas as pl
from jax.experimental.pallas import tpu as pltpu
from jax.sharding import Mesh
from jax.sharding import PartitionSpec as P

ITERS = 3
TILE = 512
WORDS = TILE // 32
SPAN = 5
ROWS = ("z", "y", "x", "core")
KIND = jnp.float8_e4m3fn


def unpack_words(words):
    shifts = lax.broadcasted_iota(jnp.int32, (WORDS, 32, TILE), 1)
    spread = jnp.broadcast_to(words[:, None, :], (WORDS, 32, TILE))
    bits = (spread >> shifts) & 1
    return bits.reshape(TILE, TILE).astype(jnp.float32)


def peel_kernel(core_ref, thresh_ref, far_ref, chip_ref, near_ref, out_ref, count_ref, band_a, band_b):
    first = core_ref[0] == 0
    thresh = thresh_ref[0].astype(jnp.float32)

    def block(ref, p, q):
        return ref.at[p * TILE : (p + 1) * TILE, q * TILE : (q + 1) * TILE]

    def piece(index):
        def rows(parts):
            at = index * WORDS
            for ref in parts:
                if at < ref.shape[0]:
                    return ref[at : at + WORDS, :]
                at -= ref.shape[0]

        left = rows((far_ref, chip_ref, near_ref))
        right = rows((near_ref, chip_ref, far_ref))
        return jnp.where(first, left, right)

    row_ids = lax.broadcasted_iota(jnp.int32, (TILE, TILE), 0)
    col_ids = lax.broadcasted_iota(jnp.int32, (TILE, TILE), 1)
    for index in range(8):
        tile = unpack_words(piece(index))
        p = (index + 1) // 2
        if index % 2:
            upper = jnp.where(col_ids > row_ids, tile, 0.0)
            block(band_a, p, p)[...] = (upper + upper.T).astype(KIND)
        else:
            block(band_a, p, p + 1)[...] = tile.astype(KIND)
            block(band_a, p + 1, p)[...] = tile.T.astype(KIND)

    def total(ref, p, q):
        ones = jnp.ones((32, TILE), KIND)
        sums = jnp.dot(ones, block(ref, p, q)[...], preferred_element_type=jnp.float32)
        return jnp.sum(sums[:8], axis=1, keepdims=True)

    def support(ref, p, q):
        lo = min(p, q) - (p == q)
        hi = max(p, q) + (p == q)
        lhs = ref[p * TILE : (p + 1) * TILE, lo * TILE : (hi + 1) * TILE]
        rhs = ref[lo * TILE : (hi + 1) * TILE, q * TILE : (q + 1) * TILE]
        return jnp.dot(lhs, rhs, preferred_element_type=jnp.float32)

    old, new = band_a, band_b
    sums = [(total(old, 2, 2), total(old, 2, 3))]
    for step in range(ITERS):
        for index in range(1 + step, 7 - step):
            p = (index + 1) // 2
            q = p + (index + 1) % 2
            counts = support(old, p, q)
            mask = block(old, p, q)[...].astype(jnp.float32)
            kept = jnp.where(counts >= thresh, mask, 0.0)
            block(new, p, q)[...] = kept.astype(KIND)
            if p != q and step < ITERS - 1:
                block(new, q, p)[...] = kept.T.astype(KIND)
            if step == ITERS - 1:
                out_ref[:, (q - 2) * TILE : (q - 1) * TILE] = counts * kept
        sums.append((total(new, 2, 2), total(new, 2, 3)))
        old, new = new, old

    lane = lax.broadcasted_iota(jnp.int32, (8, 128), 1)
    removed = jnp.zeros((8, 128), jnp.float32)
    for step in range(ITERS):
        within = (sums[step][0] - sums[step + 1][0]) * 0.5
        across = sums[step][1] - sums[step + 1][1]
        removed = jnp.where(lane == step, within + across, removed)
    count_ref[...] = removed.astype(jnp.int32)


def peel(core, thresh, far, chip, near):
    vmem = pl.BlockSpec(memory_space=pltpu.VMEM)
    smem = pl.BlockSpec(memory_space=pltpu.SMEM)
    return pl.pallas_call(
        peel_kernel,
        out_shape=(
            jax.ShapeDtypeStruct((TILE, 2 * TILE), jnp.float32),
            jax.ShapeDtypeStruct((8, 128), jnp.int32),
        ),
        in_specs=[smem, smem, vmem, vmem, vmem],
        out_specs=(vmem, vmem),
        scratch_shapes=[
            pltpu.VMEM((SPAN * TILE, SPAN * TILE), KIND),
            pltpu.VMEM((SPAN * TILE, SPAN * TILE), KIND),
        ],
        compiler_params=pltpu.CompilerParams(vmem_limit_bytes=60 * 1024 * 1024),
    )(core, thresh, far, chip, near)


def gather_sum(values, axes, members):
    spread = jnp.broadcast_to(values[None], (members,) + values.shape)
    return jnp.sum(lax.all_to_all(spread, axes, 0, 0), axis=0)


def on_device(adj_diag, adj_right, alive_diag, alive_right, truss_k):
    count = lax.axis_size(ROWS)
    core = lax.axis_index("core")
    within = adj_diag & alive_diag
    across = adj_right & alive_right
    near = lax.ppermute(
        jnp.where(core == 0, within, across),
        ROWS,
        [(i, (i + 2 if i % 2 else i - 2) % count) for i in range(count)],
    )
    chip = lax.all_gather(jnp.concatenate([within, across], axis=0), "core", tiled=True)
    far = lax.ppermute(
        jnp.where(core == 0, chip[: 3 * WORDS], chip[WORDS:]),
        ROWS,
        [(i, (i + 1 if i % 2 else i - 1) % count) for i in range(count)],
    )
    support, removed = peel(core.reshape(1), truss_k - 2, far, chip, near)
    removed = gather_sum(removed[0, :ITERS], ("y", "core"), 16)
    removed = gather_sum(removed, ("z", "x"), 32)
    return (support, removed)


def solution(mesh):
    split = Mesh(mesh.devices.reshape(8, 8, 4, 2), ROWS)
    placed = (P(ROWS, None), P(ROWS, None), P(ROWS, None), P(ROWS, None), P())
    return jax.shard_map(
        on_device, mesh=split, in_specs=placed, out_specs=(P(ROWS, None), P()), check_vma=False
    )
```

time: 129 us -> 61.2 us (0.47)
  starting transfers between devices: 33.7 us -> 3.84 us
  local copies, waits for them, and re-layouts: 20.4 us -> 1.34 us
  matrix products: 14.6 us -> 0 us
  other arithmetic: 13.6 us -> 1.43 us
  between operations: 11.1 us -> 1.33 us
  waiting for transfers between devices: 0.02 us -> 9.15 us
  Pallas kernels: 0 us -> 7.65 us
    psum x4 -> x0, blocking collectives: 35 us -> none  [over_axes(): array = lax.psum(array, axis)]
    ppermute x6 -> x2, starting transfers between devices: 33.7 us -> 3.84 us  [the longest x1 1.92 us: on_device(): lax.ppermute(jnp.where(core == 0, chip[:3 * WORDS], chip[WORDS:]), ROWS,...]
    all_to_all x0 -> x2, blocking collectives: none -> 27.7 us  [gather_sum(): return jnp.sum(lax.all_to_all(spread, axes, 0, 0), axis=0)]
    dot_general x15 -> x0, matrix products: 14.6 us -> none  [the longest x3 6.13 us: support_across(): jnp.dot(across, next_within, preferred_element_type=jnp.float32)]
    rev x6 -> x0, local copies, waits for them, and re-layouts: 11.1 us -> none  [the longest x3 8.42 us: unfold_within(): jnp.where(col_ids < row_ids, folded, jnp.zeros_like(folded))[::-1, ::-1]]
    ppermute x6 -> x2, waiting for transfers between devices: 0.02 us -> 9.15 us  [the longest x1 9.14 us: on_device(): lax.ppermute(jnp.where(core == 0, within, across), ROWS, [(i, (i + 2 if i...]
    all_gather x0 -> x1, blocking collectives: none -> 8.38 us  [on_device(): lax.all_gather(jnp.concatenate([within, across], axis=0), 'core', tiled=T...]
    concatenate x3 -> x0, local copies, waits for them, and re-layouts: 7.69 us -> none  [unfold_within(): upper_half = jnp.concatenate([top_rows, bottom_rows], axis=0)]
  transfers between devices with their start and end apart: 6 -> 2, of which waited for: 0 -> 1; matrix products, arithmetic and copies ran while one was open for 21% -> 0% of each run, Pallas kernels for 0% -> 0%
where the time goes in v1:
time: 61.2 us; the launch traced here: 60.8 us
  blocking collectives  36.1 us (59%)
  waiting for transfers between devices  9.15 us (15%)
  Pallas kernels  7.65 us (12%)
  starting transfers between devices  3.84 us (6%)
  other arithmetic  1.43 us (2%)
  local copies, waits for them, and re-layouts  1.34 us (2%)
  between operations  1.33 us (2%)
    all_to_all x2, blocking collectives, gather_sum(): return jnp.sum(lax.all_to_all(spread, axes, 0, 0), axis=0)  27.7 us
    ppermute x1, waiting for transfers between devices, on_device(): lax.ppermute(jnp.where(core == 0, within, across), ROWS, [(i, (i + 2 if i...  9.14 us
    all_gather x1, blocking collectives, on_device(): lax.all_gather(jnp.concatenate([within, across], axis=0), 'core', tiled=T...  8.38 us
    pallas_call x1, Pallas kernels, peel(): pl.pallas_call(peel_kernel, out_shape=(jax.ShapeDtypeStruct((TILE, 2 * TI...  7.65 us
    ppermute x1, starting transfers between devices, on_device(): lax.ppermute(jnp.where(core == 0, chip[:3 * WORDS], chip[WORDS:]), ROWS,...  1.92 us
    ppermute x1, starting transfers between devices, on_device(): lax.ppermute(jnp.where(core == 0, within, across), ROWS, [(i, (i + 2 if i...  1.92 us
  transfers between devices with their start and end apart: 2, of which 1 were waited for; matrix products, arithmetic and copies ran while one was open for 0% of the time, Pallas kernels for 0%

profile of v1, /device:TPU:1, one launch (start us, length us, event | category | flops | bytes accessed | tf_op | source)
XLA Modules:
  0.0 60.8 jit_solution(9467590373245150520)
XLA Ops:
  0.6 0.8 %broadcast_select_fusion = (s32[16,512]{1,0:T(8,128)S(1)}, s32[16,512]{1,0:T(8,128)S(1)}, s32[16,512]{1,0:T(8,128)S(1)}) fusion(pred[]{:T(512)S(6)} %eq.4, s32[16,512]{1,0:T(8,128)} %param.5, s32[16,512]{1,0:T(8,128)} %param.7, s32[16,512]{1,0:T(8,128)} %param.6, s32[16,512]{1,0:T(8,128)} %param.8), kind=kLoop, calls=%fused_computation.2 | loop fusion | flops 24576 | bytes 229377 | tf_op jit(solution)/shard_map/jit(_where)/select_n | solution.py:123
  1.5 8.4 %all_gather.3.chip_ref = s32[64,512]{1,0:T(8,128)S(1)} all-gather(s32[32,512]{1,0:T(8,128)S(1)} %pad_add_fusion), channel_id=1, replica_groups=mesh['z'=8,'y'=8,'x'=4,'core'=2] {'core'}, dimensions={0}, use_global_device_ids=true | all-gather | bytes 196608 | tf_op jit(solution)/shard_map/all_gather | solution.py:127
  9.9 0.0 copy-start
  9.9 1.9 %collective-permute-start = (s32[48,512]{1,0:T(8,128)S(1)}, s32[48,512]{1,0:T(8,128)S(1)}, u32[]{:S(2)}, u32[]{:S(2)}) collective-permute-start(s32[48,512]{1,0:T(8,128)S(1)} %slice_select_fusion), channel_id=1, source_target_pairs={{0,511},{1,2},{2,1},{3,4},{4,3},{5,6},{6,5},{7,8},{8,7},{9,10},{10... | collective-permute-start | bytes 294920 | tf_op jit(solution)/shard_map/ppermute | solution.py:128
  11.8 1.9 %collective-permute-start.1 = (s32[16,512]{1,0:T(8,128)S(1)}, s32[16,512]{1,0:T(8,128)S(1)}, u32[]{:S(2)}, u32[]{:S(2)}) collective-permute-start(s32[16,512]{1,0:T(8,128)S(1)} %get-tuple-element.6), channel_id=1, source_target_pairs={{0,510},{1,3},{2,0},{3,5},{4,2},{5,7},{6,4},{7,9},{8,6},{9,11},{10... | collective-permute-start | bytes 98312 | tf_op jit(solution)/shard_map/ppermute | solution.py:122
  14.4 9.1 %collective-permute-done.1.near_ref = s32[16,512]{1,0:T(8,128)S(1)} collective-permute-done((s32[16,512]{1,0:T(8,128)S(1)}, s32[16,512]{1,0:T(8,128)S(1)}, u32[]{:S(2)}, u32[]{:S(2)}) %collective-permute-start.1) | collective-permute-done | bytes 32800 | tf_op jit(solution)/shard_map/ppermute | solution.py:122
  23.5 0.0 copy-start.2
  23.5 0.0 collective-permute-done.far_ref
  23.5 0.0 copy-start.1
  23.5 0.0 copy-done
  23.5 0.6 copy-done.2
  24.1 0.0 copy-done.1
  24.2 7.6 %shard_map.68 = (f32[512,1024]{1,0:T(8,128)}, s32[8,128]{1,0:T(8,128)}) custom-call(s32[1]{0:T(128)} %bitcast.core_ref, s32[1]{0:T(128)S(6)} %sub.3.thresh_ref, s32[48,512]{1,0:T(8,128)} %copy-done.1, s32[64,512]{1,0:T(8,128)} %copy-done, s32[16,512]{1,0:T(8,128)} %copy-done.2), custom_call_target="tpu_custom_call" | custom-call | tf_op jit(solution)/shard_map/pallas_call | solution.py:96
  31.8 0.7 %slice_bitcast_fusion = s32[3]{0:T(128)S(1)} fusion(s32[8,128]{1,0:T(8,128)} %get-tuple-element.5), kind=kLoop, calls=%fused_computation.3 | loop fusion | bytes 24 | tf_op jit(solution)/shard_map/slice | solution.py:134
  32.5 12.4 %all_to_all.12 = s32[16,1,3]{2,1,0:T(1,128)S(1)} all-to-all(s32[16,1,3]{2,1,0:T(1,128)S(1)} %broadcast_in_dim.4), channel_id=1, replica_groups=mesh['z'=8,'y'=8,'x'=4,'core'=2] {'y','core'}, dimensions={0} | all-to-all | bytes 384 | tf_op jit(solution)/shard_map/all_to_all | solution.py:114
  45.0 15.3 %all_to_all.13 = s32[32,1,3]{2,1,0:T(1,128)S(1)} all-to-all(s32[32,1,3]{2,1,0:T(1,128)S(1)} %broadcast_in_dim.5), channel_id=1, replica_groups=mesh['z'=8,'y'=8,'x'=4,'core'=2] {'z','x'}, dimensions={0} | all-to-all | bytes 768 | tf_op jit(solution)/shard_map/all_to_all | solution.py:114
  60.3 0.6 reduce_sum.19
  (5 shorter events, 0.1 us)
Async XLA Ops:
  9.9 13.7 %copy-start = (s32[64,512]{1,0:T(8,128)}, s32[64,512]{1,0:T(8,128)S(1)}, u32[]{:S(2)}) copy-start(s32[64,512]{1,0:T(8,128)S(1)} %all_gather.3.chip_ref) | copy-start | bytes 393220
  9.9 13.7 %collective-permute-start = (s32[48,512]{1,0:T(8,128)S(1)}, s32[48,512]{1,0:T(8,128)S(1)}, u32[]{:S(2)}, u32[]{:S(2)}) collective-permute-start(s32[48,512]{1,0:T(8,128)S(1)} %slice_select_fusion), channel_id=1, source_target_pairs={{0,511},{1,2},{2,1},{3,4},{4,3},{5,6},{6,5},{7,8},{8,7},{9,10},{10... | collective-permute-start | bytes 294920 | tf_op jit(solution)/shard_map/ppermute | solution.py:128
  11.8 11.7 %collective-permute-start.1 = (s32[16,512]{1,0:T(8,128)S(1)}, s32[16,512]{1,0:T(8,128)S(1)}, u32[]{:S(2)}, u32[]{:S(2)}) collective-permute-start(s32[16,512]{1,0:T(8,128)S(1)} %get-tuple-element.6), channel_id=1, source_target_pairs={{0,510},{1,3},{2,0},{3,5},{4,2},{5,7},{6,4},{7,9},{8,6},{9,11},{10... | collective-permute-start | bytes 98312 | tf_op jit(solution)/shard_map/ppermute | solution.py:122
  23.5 0.6 copy-start.2
  23.5 0.6 %copy-start.1 = (s32[48,512]{1,0:T(8,128)}, s32[48,512]{1,0:T(8,128)S(1)}, u32[]{:S(2)}) copy-start(s32[48,512]{1,0:T(8,128)S(1)} %collective-permute-done.far_ref) | copy-start | bytes 294916

commit v2 on v1

v2 whole, which is shorter than its diff:
```python
import functools

import jax
import jax.numpy as jnp
from jax import lax
from jax.experimental import pallas as pl
from jax.experimental.pallas import tpu as pltpu
from jax.sharding import Mesh
from jax.sharding import PartitionSpec as P

ITERS = 3
TILE = 512
HALF = TILE // 2
WORDS = TILE // 32
SIDE = 128
ROWS = ("z", "y", "x", "core")
FIRST = ("y", "core")
SECOND = ("z", "x")
KIND = jnp.float8_e4m3fn
WIDE = jnp.bfloat16
MIB = 1024 * 1024


def unpack(words):
    rows, width = words.shape
    shifts = lax.broadcasted_iota(jnp.int32, (rows, 32, width), 1)
    spread = jnp.broadcast_to(words[:, None, :], (rows, 32, width))
    return ((spread >> shifts) & 1).reshape(rows * 32, width).astype(jnp.float32)


def fill_within(words, ref):
    row_ids = lax.broadcasted_iota(jnp.int32, (SIDE, SIDE), 0)
    col_ids = lax.broadcasted_iota(jnp.int32, (SIDE, SIDE), 1)
    for at in range(0, TILE, SIDE):
        stripe = unpack(words[at // 32 : (at + SIDE) // 32, at:])
        corner = jnp.where(col_ids > row_ids, stripe[:, :SIDE], 0.0)
        flipped = corner.astype(KIND).T.astype(jnp.float32)
        ref[at : at + SIDE, at : at + SIDE] = (corner + flipped).astype(KIND)
        if at + SIDE < TILE:
            rest = stripe[:, SIDE:].astype(KIND)
            ref[at : at + SIDE, at + SIDE :] = rest
            ref[at + SIDE :, at : at + SIDE] = rest.T


def fill_across(words, ref, ref_t):
    tile = unpack(words).astype(KIND)
    ref[...] = tile
    ref_t[...] = tile.T


def times(lhs, rhs):
    return jnp.dot(lhs, rhs, preferred_element_type=jnp.float32)


def inside(left, left_t, here, right, right_t, rows, cols):
    return (
        times(left_t[rows, :], left[:, cols])
        + times(here[rows, :], here[:, cols])
        + times(right[rows, :], right_t[:, cols])
    )


def between(left, here, right, rows):
    return times(left[rows, :], here[...]) + times(here[rows, :], right[...])


def keep(counts, old, thresh):
    return jnp.where(counts.astype(WIDE) >= thresh, old.astype(WIDE), jnp.zeros((), WIDE)).astype(KIND)


TOP, LOW = slice(0, HALF), slice(HALF, TILE)
ALL = slice(0, TILE)


def peel_within(left, left_t, here, right, right_t, thresh, new):
    kept = keep(inside(left, left_t, here, right, right_t, TOP, ALL), here[TOP, :], thresh)
    new[TOP, :] = kept
    new[LOW, TOP] = kept[:, HALF:].T
    new[LOW, LOW] = keep(inside(left, left_t, here, right, right_t, LOW, LOW), here[LOW, LOW], thresh)


def peel_across(left, here, right, thresh, new, new_t):
    for rows in (TOP, LOW):
        kept = keep(between(left, here, right, rows), here[rows, :], thresh)
        new[rows, :] = kept
        new_t[:, rows] = kept.T


def chip_kernel(thresh_ref, chip_ref, tiles_ref):
    thresh = thresh_ref[0].astype(jnp.float32).astype(WIDE)
    w0, a0, a0_t, w1, a1, a1_t, new_a0, new_a0_t, new_w1 = (tiles_ref.at[i] for i in range(9))
    fill_within(chip_ref[:WORDS, :], w0)
    fill_across(chip_ref[WORDS : 2 * WORDS, :], a0, a0_t)
    fill_within(chip_ref[2 * WORDS : 3 * WORDS, :], w1)
    fill_across(chip_ref[3 * WORDS :, :], a1, a1_t)
    peel_across(w0, a0, w1, thresh, new_a0, new_a0_t)
    peel_within(a0, a0_t, w1, a1, a1_t, thresh, new_w1)


def edges(ref):
    tile = ref[...].astype(WIDE)
    parts = [tile[at : at + 32, :] for at in range(0, TILE, 32)]
    while len(parts) > 1:
        parts = [parts[i] + parts[i + 1] for i in range(0, len(parts), 2)]
    return parts[0].astype(jnp.float32)


def peel_kernel(core_ref, thresh_ref, far_ref, near_ref, chip_ref, out_ref, count_ref, pool):
    def body(core):
        level = thresh_ref[0].astype(jnp.float32)
        thresh = level.astype(WIDE)
        slots = iter(range(pool.shape[0]))

        def fresh():
            return pool.at[next(slots)]

        w0, a0, a0_t, w1, a1, a1_t, new_a0, new_a0_t, new_w1 = (chip_ref.at[i] for i in range(9))
        shift = 3 - 2 * core
        now = {shift: (w0,), shift + 1: (a0, a0_t), shift + 2: (w1,), shift + 3: (a1, a1_t)}
        new = {shift + 1: (new_a0, new_a0_t), shift + 2: (new_w1,)}

        def words(index):
            at = index - 5 * core
            if 0 <= at < 3:
                return far_ref[at * WORDS : (at + 1) * WORDS, :]
            return near_ref[...]

        for index in range(8):
            if index not in now and index % 2:
                now[index] = (fresh(),)
                fill_within(words(index), *now[index])
            elif index not in now:
                now[index] = (fresh(), fresh())
                fill_across(words(index), *now[index])

        total = [edges(now[3][0]) * 0.5 + edges(now[4][0])]
        for step in range(ITERS - 1):
            for index in range(1 + step, 7 - step):
                if index in new:
                    continue
                left, here, right = now[index - 1], now[index], now[index + 1]
                if index % 2:
                    new[index] = (fresh(),)
                    peel_within(*left, *here, *right, thresh, *new[index])
                else:
                    new[index] = (fresh(), fresh())
                    peel_across(left[0], here[0], right[0], thresh, *new[index])
            now, new = new, {}
            total.append(edges(now[3][0]) * 0.5 + edges(now[4][0]))

        last = jnp.zeros((8, TILE), jnp.float32)
        for rows in (TOP, LOW):
            counts = inside(*now[2], *now[3], *now[4], rows, ALL)
            kept = jnp.where(counts >= level, now[3][0][rows, :].astype(jnp.float32), 0.0)
            out_ref[rows, :TILE] = counts * kept
            last = last + 0.5 * jnp.sum(kept.reshape(HALF // 8, 8, TILE), axis=0)
            counts = between(*now[3], now[4][0], *now[5], rows)
            kept = jnp.where(counts >= level, now[4][0][rows, :].astype(jnp.float32), 0.0)
            out_ref[rows, TILE:] = counts * kept
            last = last + jnp.sum(kept.reshape(HALF // 8, 8, TILE), axis=0)

        sums = [jnp.sum(part) for part in total] + [jnp.sum(last)]
        lane = lax.broadcasted_iota(jnp.int32, count_ref.shape, count_ref.ndim - 1)
        removed = jnp.zeros(count_ref.shape, jnp.float32)
        for step in range(ITERS):
            removed = jnp.where(lane == step, sums[step] - sums[step + 1], removed)
        count_ref[...] = removed.astype(jnp.int32)

    for core in range(2):
        pl.when(core_ref[0] == core)(functools.partial(body, core))


VMEM = pl.BlockSpec(memory_space=pltpu.VMEM)
SMEM = pl.BlockSpec(memory_space=pltpu.SMEM)


def chip_tiles(thresh, chip):
    return pl.pallas_call(
        chip_kernel,
        out_shape=jax.ShapeDtypeStruct((9, TILE, TILE), KIND),
        in_specs=[SMEM, VMEM],
        out_specs=VMEM,
        compiler_params=pltpu.CompilerParams(vmem_limit_bytes=8 * MIB),
        cost_estimate=pl.CostEstimate(flops=10 * TILE**3, bytes_accessed=0, transcendentals=0),
    )(thresh, chip)


def peel(core, thresh, far, near, tiles):
    return pl.pallas_call(
        peel_kernel,
        out_shape=(
            pltpu.VMEM((TILE, 2 * TILE), jnp.float32),
            jax.ShapeDtypeStruct((16, 1, 128), jnp.int32),
        ),
        in_specs=[SMEM, SMEM, VMEM, VMEM, VMEM],
        out_specs=(VMEM, VMEM),
        scratch_shapes=[pltpu.VMEM((20, TILE, TILE), KIND)],
        compiler_params=pltpu.CompilerParams(vmem_limit_bytes=20 * MIB),
        cost_estimate=pl.CostEstimate(flops=50 * TILE**3, bytes_accessed=0, transcendentals=0),
    )(core, thresh, far, near, tiles)


def on_device(adj_diag, adj_right, alive_diag, alive_right, truss_k):
    count = lax.axis_size(ROWS)
    core = lax.axis_index("core")
    thresh = truss_k - 2
    within = adj_diag & alive_diag
    across = adj_right & alive_right
    near = lax.ppermute(
        jnp.where(core == 0, within, across),
        ROWS,
        [(i, (i + 2 if i % 2 else i - 2) % count) for i in range(count)],
    )
    chip = lax.all_gather(jnp.concatenate([within, across], axis=0), "core", tiled=True)
    far = lax.ppermute(
        jnp.where(core == 0, chip[: 3 * WORDS], chip[WORDS:]),
        ROWS,
        [(i, (i + 1 if i % 2 else i - 1) % count) for i in range(count)],
    )
    support, removed = peel(core.reshape(1), thresh, far, near, chip_tiles(thresh, chip))
    removed = jnp.sum(lax.all_to_all(removed, FIRST, 0, 0), axis=0, keepdims=True)
    removed = jnp.broadcast_to(removed, (32, 1, 128))
    removed = jnp.sum(lax.all_to_all(removed, SECOND, 0, 0), axis=(0, 1))
    return (support, removed[:ITERS])


def solution(mesh):
    split = Mesh(mesh.devices.reshape(8, 8, 4, 2), ROWS)
    placed = (P(ROWS, None), P(ROWS, None), P(ROWS, None), P(ROWS, None), P())
    return jax.shard_map(
        on_device, mesh=split, in_specs=placed, out_specs=(P(ROWS, None), P()), check_vma=False
    )
```

time: 61.2 us -> 59.3 us (0.969)
  starting transfers between devices: 3.84 us -> 9.63 us
  blocking collectives: 36.1 us -> 30.5 us
  Pallas kernels: 7.65 us -> 4.81 us
    all_to_all x2 -> x1, blocking collectives: 27.7 us -> 15.4 us  [on_device(): lax.all_to_all(removed, FIRST, 0, 0)]
    ppermute x1, waiting for transfers between devices: 9.14 us -> 0.01 us  [on_device(): lax.ppermute(jnp.where(core == 0, within, across), ROWS, [(i, (i + 2 if i...]
    all_to_all x0 -> x1, waiting for transfers between devices: none -> 7.13 us  [on_device(): removed = jnp.sum(lax.all_to_all(removed, SECOND, 0, 0), axis=(0, 1))]
    all_gather x1, blocking collectives: 8.38 us -> 15.1 us  [on_device(): lax.all_gather(jnp.concatenate([within, across], axis=0), 'core', tiled=T...]
    all_to_all x0 -> x1, starting transfers between devices: none -> 3.77 us  [on_device(): removed = jnp.sum(lax.all_to_all(removed, SECOND, 0, 0), axis=(0, 1))]
    pallas_call x1 -> x2, Pallas kernels: 7.65 us -> 4.81 us  [the longest x1 3.66 us: peel(): pl.pallas_call(peel_kernel, out_shape=(pltpu.VMEM((TILE, 2 * TILE), jnp.f...]
    ppermute x1, waiting for transfers between devices: 0.01 us -> 2.21 us  [on_device(): lax.ppermute(jnp.where(core == 0, chip[:3 * WORDS], chip[WORDS:]), ROWS,...]
    ppermute x1, starting transfers between devices: 1.92 us -> 3.94 us  [on_device(): lax.ppermute(jnp.where(core == 0, within, across), ROWS, [(i, (i + 2 if i...]
  transfers between devices with their start and end apart: 2 -> 3, of which waited for: 1 -> 2; matrix products, arithmetic and copies ran while one was open for 0% -> 2% of each run, Pallas kernels for 0% -> 2%
where the time goes in v2:
time: 59.3 us; the launch traced here: 59 us
  blocking collectives  30.5 us (51%)
  starting transfers between devices  9.63 us (16%)
  waiting for transfers between devices  9.34 us (16%)
  Pallas kernels  4.81 us (8%)
  local copies, waits for them, and re-layouts  1.93 us (3%)
  other arithmetic  1.4 us (2%)
  between operations  1.34 us (2%)
    all_to_all x1, blocking collectives, on_device(): lax.all_to_all(removed, FIRST, 0, 0)  15.4 us
    all_gather x1, blocking collectives, on_device(): lax.all_gather(jnp.concatenate([within, across], axis=0), 'core', tiled=T...  15.1 us
    all_to_all x1, waiting for transfers between devices, on_device(): removed = jnp.sum(lax.all_to_all(removed, SECOND, 0, 0), axis=(0, 1))  7.13 us
    ppermute x1, starting transfers between devices, on_device(): lax.ppermute(jnp.where(core == 0, within, across), ROWS, [(i, (i + 2 if i...  3.94 us
    all_to_all x1, starting transfers between devices, on_device(): removed = jnp.sum(lax.all_to_all(removed, SECOND, 0, 0), axis=(0, 1))  3.77 us
    pallas_call x1, Pallas kernels, peel(): pl.pallas_call(peel_kernel, out_shape=(pltpu.VMEM((TILE, 2 * TILE), jnp.f...  3.66 us
    ppermute x1, waiting for transfers between devices, on_device(): lax.ppermute(jnp.where(core == 0, chip[:3 * WORDS], chip[WORDS:]), ROWS,...  2.21 us
    ppermute x1, starting transfers between devices, on_device(): lax.ppermute(jnp.where(core == 0, chip[:3 * WORDS], chip[WORDS:]), ROWS,...  1.92 us
  transfers between devices with their start and end apart: 3, of which 2 were waited for; matrix products, arithmetic and copies ran while one was open for 2% of the time, Pallas kernels for 2%

profile of v2, /device:TPU:1, one launch (start us, length us, event | category | flops | bytes accessed | tf_op | source)
XLA Modules:
  0.0 59.0 jit_solution(10350925707978755709)
XLA Ops:
  0.6 0.8 %broadcast_select_fusion = (s32[16,512]{1,0:T(8,128)S(1)}, s32[16,512]{1,0:T(8,128)S(1)}, s32[16,512]{1,0:T(8,128)S(1)}) fusion(pred[]{:T(512)S(6)} %eq.4, s32[16,512]{1,0:T(8,128)} %param.5, s32[16,512]{1,0:T(8,128)} %param.7, s32[16,512]{1,0:T(8,128)} %param.6, s32[16,512]{1,0:T(8,128)} %param.8), kind=kLoop, calls=%fused_computation.2 | loop fusion | flops 24576 | bytes 229377 | tf_op jit(solution)/shard_map/jit(_where)/select_n | solution.py:210
  1.5 3.9 %collective-permute-start.1 = (s32[16,512]{1,0:T(8,128)S(1)}, s32[16,512]{1,0:T(8,128)S(1)}, u32[]{:S(2)}, u32[]{:S(2)}) collective-permute-start(s32[16,512]{1,0:T(8,128)S(1)} %get-tuple-element.6), channel_id=1, source_target_pairs={{0,510},{1,3},{2,0},{3,5},{4,2},{5,7},{6,4},{7,9},{8,6},{9,11},{10... | collective-permute-start | bytes 98312 | tf_op jit(solution)/shard_map/ppermute | solution.py:209
  5.4 15.1 %all_gather.3.chip_ref = s32[64,512]{1,0:T(8,128)S(1)} all-gather(s32[32,512]{1,0:T(8,128)S(1)} %pad_add_fusion), channel_id=1, replica_groups=mesh['z'=8,'y'=8,'x'=4,'core'=2] {'core'}, dimensions={0}, use_global_device_ids=true | all-gather | bytes 196608 | tf_op jit(solution)/shard_map/all_gather | solution.py:214
  20.6 1.9 %collective-permute-start = (s32[48,512]{1,0:T(8,128)S(1)}, s32[48,512]{1,0:T(8,128)S(1)}, u32[]{:S(2)}, u32[]{:S(2)}) collective-permute-start(s32[48,512]{1,0:T(8,128)S(1)} %slice_select_fusion), channel_id=1, source_target_pairs={{0,511},{1,2},{2,1},{3,4},{4,3},{5,6},{6,5},{7,8},{8,7},{9,10},{10... | collective-permute-start | bytes 294920 | tf_op jit(solution)/shard_map/ppermute | solution.py:215
  23.2 1.1 %shard_map.68.chip_ref = f8e4m3fn[9,512,512]{2,1,0:T(32,128)(4,1)S(1)} custom-call(s32[1]{0:T(128)S(6)} %sub.3.thresh_ref, s32[64,512]{1,0:T(8,128)S(1)} %all_gather.3.chip_ref), custom_call_target="tpu_custom_call" | custom-call | flops 1342177280 | tf_op jit(solution)/shard_map/pallas_call | solution.py:178
  24.3 0.0 collective-permute-done.1.near_ref
  24.3 2.2 %collective-permute-done.far_ref = s32[48,512]{1,0:T(8,128)S(1)} collective-permute-done((s32[48,512]{1,0:T(8,128)S(1)}, s32[48,512]{1,0:T(8,128)S(1)}, u32[]{:S(2)}, u32[]{:S(2)}) %collective-permute-start) | collective-permute-done | bytes 98336 | tf_op jit(solution)/shard_map/ppermute | solution.py:215
  26.5 3.7 %shard_map.69 = (f32[512,1024]{1,0:T(8,128)S(1)}, s32[16,1,128]{2,1,0:T(1,128)S(1)}) custom-call(s32[1]{0:T(128)} %bitcast.core_ref, s32[1]{0:T(128)S(6)} %sub.3.thresh_ref, s32[48,512]{1,0:T(8,128)S(1)} %collective-permute-done.far_ref, s32[16,512]{1,0:T(8,128)S(1)} %collective-permute-done.1.near_ref, f8e4m3fn[9,512,512]{2,1,0:T(32,128)(4,1)S(1)} %shard_map.68.chip_ref), custom_call_target="tpu_custom_call" | custom-call | flops 6710886400 | tf_op jit(solution)/shard_map/pallas_call | solution.py:189
  30.2 15.4 %all_to_all.10 = s32[16,1,128]{2,1,0:T(1,128)S(1)} all-to-all(s32[16,1,128]{2,1,0:T(1,128)S(1)} %get-tuple-element.5), channel_id=1, replica_groups=mesh['z'=8,'y'=8,'x'=4,'core'=2] {'y','core'}, dimensions={0} | all-to-all | bytes 16384 | tf_op jit(solution)/shard_map/all_to_all | solution.py:221
  45.6 0.6 %broadcast_in_dim.2 = s32[32,1,128]{2,1,0:T(1,128)} broadcast(s32[128]{0:T(128)S(1)} %reduce_sum.18), dimensions={2} | broadcast | bytes 16896 | tf_op jit(solution)/shard_map/broadcast_in_dim | solution.py:222
  46.2 3.8 %all-to-all-start.1 = ((s32[32,1,128]{2,1,0:T(1,128)}), s32[32,1,128]{2,1,0:T(1,128)S(1)}, u32[]{:S(2)}, u32[]{:S(2)}) async-start(s32[32,1,128]{2,1,0:T(1,128)} %broadcast_in_dim.2), calls=%async_computation.1 | async-start | bytes 32768 | tf_op jit(solution)/shard_map/all_to_all | solution.py:223
  50.0 1.3 %copy.8 = f32[512,1024]{1,0:T(8,128)} copy(f32[512,1024]{1,0:T(8,128)S(1)} %get-tuple-element.9) | data formatting | bytes 4194304
  51.3 7.1 %all-to-all-done.1 = s32[32,1,128]{2,1,0:T(1,128)S(1)} async-done(((s32[32,1,128]{2,1,0:T(1,128)}), s32[32,1,128]{2,1,0:T(1,128)S(1)}, u32[]{:S(2)}, u32[]{:S(2)}) %all-to-all-start.1) | async-done | bytes 16416 | tf_op jit(solution)/shard_map/all_to_all | solution.py:223
  58.5 0.5 reduce_sum.19
  (3 shorter events, 0.1 us)
Async XLA Ops:
  1.5 22.8 %collective-permute-start.1 = (s32[16,512]{1,0:T(8,128)S(1)}, s32[16,512]{1,0:T(8,128)S(1)}, u32[]{:S(2)}, u32[]{:S(2)}) collective-permute-start(s32[16,512]{1,0:T(8,128)S(1)} %get-tuple-element.6), channel_id=1, source_target_pairs={{0,510},{1,3},{2,0},{3,5},{4,2},{5,7},{6,4},{7,9},{8,6},{9,11},{10... | collective-permute-start | bytes 98312 | tf_op jit(solution)/shard_map/ppermute | solution.py:209
  20.6 5.9 %collective-permute-start = (s32[48,512]{1,0:T(8,128)S(1)}, s32[48,512]{1,0:T(8,128)S(1)}, u32[]{:S(2)}, u32[]{:S(2)}) collective-permute-start(s32[48,512]{1,0:T(8,128)S(1)} %slice_select_fusion), channel_id=1, source_target_pairs={{0,511},{1,2},{2,1},{3,4},{4,3},{5,6},{6,5},{7,8},{8,7},{9,10},{10... | collective-permute-start | bytes 294920 | tf_op jit(solution)/shard_map/ppermute | solution.py:215
  46.2 12.2 %all-to-all-start.1 = ((s32[32,1,128]{2,1,0:T(1,128)}), s32[32,1,128]{2,1,0:T(1,128)S(1)}, u32[]{:S(2)}, u32[]{:S(2)}) async-start(s32[32,1,128]{2,1,0:T(1,128)} %broadcast_in_dim.2), calls=%async_computation.1 | async-start | bytes 32768 | tf_op jit(solution)/shard_map/all_to_all | solution.py:223

commit v3 on v2

--- a/solution.py
+++ b/solution.py
@@ -7,6 +7,7 @@
 from jax.experimental.pallas import tpu as pltpu
 from jax.sharding import Mesh
 from jax.sharding import PartitionSpec as P
+
 
 ITERS = 3
 TILE = 512
@@ -105,69 +106,100 @@
     return parts[0].astype(jnp.float32)
 
 
-def peel_kernel(core_ref, thresh_ref, far_ref, near_ref, chip_ref, out_ref, count_ref, pool):
+def chip_levels(chip_ref, core):
+    w0, a0, a0_t, w1, a1, a1_t, new_a0, new_a0_t, new_w1 = (chip_ref.at[i] for i in range(9))
+    at = 3 - 2 * core
+    start = {at: (w0,), at + 1: (a0, a0_t), at + 2: (w1,), at + 3: (a1, a1_t)}
+    return start, {at + 1: (new_a0, new_a0_t), at + 2: (new_w1,)}
+
+
+def fresh_tiles(pool):
+    slots = iter(range(pool.shape[0]))
+    return lambda index: tuple(pool.at[next(slots)] for _ in range(2 - index % 2))
+
+
+def fill(words, index, tile):
+    (fill_within if index % 2 else fill_across)(words, *tile)
+
+
+def advance(now, index, thresh, tile):
+    left, here, right = now[index - 1], now[index], now[index + 1]
+    if index % 2:
+        peel_within(*left, *here, *right, thresh, *tile)
+    else:
+        peel_across(left[0], here[0], right[0], thresh, *tile)
+    return tile
+
+
+def finish(now, index, level, out_ref):
+    left, here, right = now[index - 1], now[index], now[index + 1]
+    cols = slice((index - 3) * TILE, (index - 2) * TILE)
+    last = jnp.zeros((8, TILE), jnp.float32)
+    for rows in (TOP, LOW):
+        if index % 2:
+            counts = inside(*left, *here, *right, rows, ALL)
+        else:
+            counts = between(left[0], here[0], right[0], rows)
+        kept = jnp.where(counts >= level, here[0][rows, :].astype(jnp.float32), 0.0)
+        out_ref[rows, cols] = counts * kept
+        last = last + jnp.sum(kept.reshape(HALF // 8, 8, TILE), axis=0)
+    return jnp.sum(last) * (0.5 if index % 2 else 1.0)
+
+
+def on_core(core_ref, body):
+    for core in range(2):
+        pl.when(core_ref[0] == core)(functools.partial(body, core))
+
+
+def main_kernel(core_ref, thresh_ref, far_ref, chip_ref, out_ref, mids_ref, sums_ref, pool):
     def body(core):
         level = thresh_ref[0].astype(jnp.float32)
         thresh = level.astype(WIDE)
-        slots = iter(range(pool.shape[0]))
-
-        def fresh():
-            return pool.at[next(slots)]
-
-        w0, a0, a0_t, w1, a1, a1_t, new_a0, new_a0_t, new_w1 = (chip_ref.at[i] for i in range(9))
-        shift = 3 - 2 * core
-        now = {shift: (w0,), shift + 1: (a0, a0_t), shift + 2: (w1,), shift + 3: (a1, a1_t)}
-        new = {shift + 1: (new_a0, new_a0_t), shift + 2: (new_w1,)}
-
-        def words(index):
-            at = index - 5 * core
-            if 0 <= at < 3:
-                return far_ref[at * WORDS : (at + 1) * WORDS, :]
-            return near_ref[...]
-
-        for index in range(8):
-            if index not in now and index % 2:
-                now[index] = (fresh(),)
-                fill_within(words(index), *now[index])
-            elif index not in now:
-                now[index] = (fresh(), fresh())
-                fill_across(words(index), *now[index])
-
-        total = [edges(now[3][0]) * 0.5 + edges(now[4][0])]
-        for step in range(ITERS - 1):
-            for index in range(1 + step, 7 - step):
-                if index in new:
-                    continue
-                left, here, right = now[index - 1], now[index], now[index + 1]
-                if index % 2:
-                    new[index] = (fresh(),)
-                    peel_within(*left, *here, *right, thresh, *new[index])
-                else:
-                    new[index] = (fresh(), fresh())
-                    peel_across(left[0], here[0], right[0], thresh, *new[index])
-            now, new = new, {}
-            total.append(edges(now[3][0]) * 0.5 + edges(now[4][0]))
-
-        last = jnp.zeros((8, TILE), jnp.float32)
-        for rows in (TOP, LOW):
-            counts = inside(*now[2], *now[3], *now[4], rows, ALL)
-            kept = jnp.where(counts >= level, now[3][0][rows, :].astype(jnp.float32), 0.0)
-            out_ref[rows, :TILE] = counts * kept
-            last = last + 0.5 * jnp.sum(kept.reshape(HALF // 8, 8, TILE), axis=0)
-            counts = between(*now[3], now[4][0], *now[5], rows)
-            kept = jnp.where(counts >= level, now[4][0][rows, :].astype(jnp.float32), 0.0)
-            out_ref[rows, TILE:] = counts * kept
-            last = last + jnp.sum(kept.reshape(HALF // 8, 8, TILE), axis=0)
-
-        sums = [jnp.sum(part) for part in total] + [jnp.sum(last)]
-        lane = lax.broadcasted_iota(jnp.int32, count_ref.shape, count_ref.ndim - 1)
-        removed = jnp.zeros(count_ref.shape, jnp.float32)
+        fresh = fresh_tiles(pool)
+        start, once = chip_levels(chip_ref, core)
+        own = {3: (mids_ref.at[0],), 4: (mids_ref.at[1], mids_ref.at[2])}
+        for slot in range(3):
+            index = slot + 5 * core
+            start[index] = fresh(index)
+            fill(far_ref[slot * WORDS : (slot + 1) * WORDS, :], index, start[index])
+        for index in range(1 + core, 6 + core):
+            if index not in once:
+                once[index] = advance(start, index, thresh, fresh(index))
+        twice = {}
+        for index in range(2 + core, 5 + core):
+            twice[index] = advance(once, index, thresh, own[index] if index in own else fresh(index))
+        total = [jnp.sum(edges(now[3][0]) * 0.5 + edges(now[4][0])) for now in (start, once, twice)]
+        total.append(finish(twice, 3 + core, level, out_ref))
+        lane = lax.broadcasted_iota(jnp.int32, sums_ref.shape, 1)
+        sums = jnp.zeros(sums_ref.shape, jnp.float32)
         for step in range(ITERS):
-            removed = jnp.where(lane == step, sums[step] - sums[step + 1], removed)
-        count_ref[...] = removed.astype(jnp.int32)
-
-    for core in range(2):
-        pl.when(core_ref[0] == core)(functools.partial(body, core))
+            sums = jnp.where(lane == step, total[step] - total[step + 1], sums)
+        sums_ref[...] = sums
+
+    on_core(core_ref, body)
+
+
+def edge_kernel(core_ref, thresh_ref, near_ref, chip_ref, mids_ref, sums_ref, _, out_ref, count_ref, pool):
+    def body(core):
+        level = thresh_ref[0].astype(jnp.float32)
+        thresh = level.astype(WIDE)
+        fresh = fresh_tiles(pool)
+        start, once = chip_levels(chip_ref, core)
+        twice = {3: (mids_ref.at[0],), 4: (mids_ref.at[1], mids_ref.at[2])}
+        step = 1 if core else -1
+        index = 0 if core else 7
+        start[index] = fresh(index)
+        fill(near_ref[...], index, start[index])
+        index += step
+        once[index] = advance(start, index, thresh, fresh(index))
+        index += step
+        twice[index] = advance(once, index, thresh, fresh(index))
+        last = finish(twice, index + step, level, out_ref)
+        sums = jnp.broadcast_to(sums_ref[:1, :][:, None, :], count_ref.shape)
+        lane = lax.broadcasted_iota(jnp.int32, count_ref.shape, 2)
+        count_ref[...] = jnp.where(lane == ITERS - 1, sums - last, sums).astype(jnp.int32)
+
+    on_core(core_ref, body)
 
 
 VMEM = pl.BlockSpec(memory_space=pltpu.VMEM)
@@ -185,19 +217,36 @@
     )(thresh, chip)
 
 
-def peel(core, thresh, far, near, tiles):
+def main_part(core, thresh, far, tiles):
     return pl.pallas_call(
-        peel_kernel,
+        main_kernel,
         out_shape=(
             pltpu.VMEM((TILE, 2 * TILE), jnp.float32),
-            jax.ShapeDtypeStruct((16, 1, 128), jnp.int32),
+            pltpu.VMEM((3, TILE, TILE), KIND),
+            pltpu.VMEM((8, 128), jnp.float32),
         ),
-        in_specs=[SMEM, SMEM, VMEM, VMEM, VMEM],
+        in_specs=[SMEM, SMEM, VMEM, VMEM],
+        out_specs=(VMEM, VMEM, VMEM),
+        scratch_shapes=[pltpu.VMEM((12, TILE, TILE), KIND)],
+        compiler_params=pltpu.CompilerParams(vmem_limit_bytes=16 * MIB),
+        cost_estimate=pl.CostEstimate(flops=36 * TILE**3, bytes_accessed=0, transcendentals=0),
+    )(core, thresh, far, tiles)
+
+
+def edge_part(core, thresh, near, tiles, mids, sums, support):
+    return pl.pallas_call(
+        edge_kernel,
+        out_shape=(
+            pltpu.VMEM((TILE, 2 * TILE), jnp.float32),
+            pltpu.VMEM((16, 1, 128), jnp.int32),
+        ),
+        in_specs=[SMEM, SMEM, VMEM, VMEM, VMEM, VMEM, VMEM],
         out_specs=(VMEM, VMEM),
-        scratch_shapes=[pltpu.VMEM((20, TILE, TILE), KIND)],
-        compiler_params=pltpu.CompilerParams(vmem_limit_bytes=20 * MIB),
-        cost_estimate=pl.CostEstimate(flops=50 * TILE**3, bytes_accessed=0, transcendentals=0),
-    )(core, thresh, far, near, tiles)
+        input_output_aliases={6: 0},
+        scratch_shapes=[pltpu.VMEM((6, TILE, TILE), KIND)],
+        compiler_params=pltpu.CompilerParams(vmem_limit_bytes=12 * MIB),
+        cost_estimate=pl.CostEstimate(flops=14 * TILE**3, bytes_accessed=0, transcendentals=0),
+    )(core, thresh, near, tiles, mids, sums, support)
 
 
 def on_device(adj_diag, adj_right, alive_diag, alive_right, truss_k):
@@ -206,18 +255,21 @@
     thresh = truss_k - 2
     within = adj_diag & alive_diag
     across = adj_right & alive_right
-    near = lax.ppermute(
-        jnp.where(core == 0, within, across),
-        ROWS,
-        [(i, (i + 2 if i % 2 else i - 2) % count) for i in range(count)],
-    )
     chip = lax.all_gather(jnp.concatenate([within, across], axis=0), "core", tiled=True)
     far = lax.ppermute(
         jnp.where(core == 0, chip[: 3 * WORDS], chip[WORDS:]),
         ROWS,
         [(i, (i + 1 if i % 2 else i - 1) % count) for i in range(count)],
     )
-    support, removed = peel(core.reshape(1), thresh, far, near, chip_tiles(thresh, chip))
+    near = lax.ppermute(
+        jnp.where(core == 0, within, across),
+        ROWS,
+        [(i, (i + 2 if i % 2 else i - 2) % count) for i in range(count)],
+    )
+    core = core.reshape(1)
+    tiles = chip_tiles(thresh, chip)
+    support, mids, sums = main_part(core, thresh, far, tiles)
+    support, removed = edge_part(core, thresh, near, tiles, mids, sums, support)
     removed = jnp.sum(lax.all_to_all(removed, FIRST, 0, 0), axis=0, keepdims=True)
     removed = jnp.broadcast_to(removed, (32, 1, 128))
     removed = jnp.sum(lax.all_to_all(removed, SECOND, 0, 0), axis=(0, 1))

time: 59.3 us -> 60.2 us (1.015)
    pallas_call x1 -> x2, Pallas kernels: 3.66 us -> 4.15 us  [the longest x1 2.77 us: main_part(): pl.pallas_call(main_kernel, out_shape=(pltpu.VMEM((TILE, 2 * TILE), jnp.f...]
  transfers between devices with their start and end apart: 3 -> 3, of which waited for: 2 -> 2; matrix products, arithmetic and copies ran while one was open for 2% -> 2% of each run, Pallas kernels for 2% -> 7%
where the time goes in v3:
time: 60.2 us; the launch traced here: 59.8 us
  blocking collectives  30.9 us (51%)
  starting transfers between devices  9.66 us (16%)
  waiting for transfers between devices  9.35 us (16%)
  Pallas kernels  5.29 us (9%)
  local copies, waits for them, and re-layouts  1.93 us (3%)
  other arithmetic  1.4 us (2%)
  between operations  1.35 us (2%)
    all_to_all x1, blocking collectives, on_device(): lax.all_to_all(removed, FIRST, 0, 0)  15.7 us
    all_gather x1, blocking collectives, on_device(): lax.all_gather(jnp.concatenate([within, across], axis=0), 'core', tiled=T...  15.1 us
    all_to_all x1, waiting for transfers between devices, on_device(): removed = jnp.sum(lax.all_to_all(removed, SECOND, 0, 0), axis=(0, 1))  7.13 us
    ppermute x1, starting transfers between devices, on_device(): lax.ppermute(jnp.where(core == 0, within, across), ROWS, [(i, (i + 2 if i...  3.94 us
    all_to_all x1, starting transfers between devices, on_device(): removed = jnp.sum(lax.all_to_all(removed, SECOND, 0, 0), axis=(0, 1))  3.8 us
    pallas_call x1, Pallas kernels, main_part(): pl.pallas_call(main_kernel, out_shape=(pltpu.VMEM((TILE, 2 * TILE), jnp.f...  2.77 us
    ppermute x1, waiting for transfers between devices, on_device(): lax.ppermute(jnp.where(core == 0, chip[:3 * WORDS], chip[WORDS:]), ROWS,...  2.21 us
    ppermute x1, starting transfers between devices, on_device(): lax.ppermute(jnp.where(core == 0, chip[:3 * WORDS], chip[WORDS:]), ROWS,...  1.92 us
  transfers between devices with their start and end apart: 3, of which 2 were waited for; matrix products, arithmetic and copies ran while one was open for 2% of the time, Pallas kernels for 7%

profile of v3, /device:TPU:1, one launch (start us, length us, event | category | flops | bytes accessed | tf_op | source)
XLA Modules:
  0.0 59.8 jit_solution(11308778216095689814)
XLA Ops:
  0.6 0.8 %broadcast_select_fusion = (s32[16,512]{1,0:T(8,128)S(1)}, s32[16,512]{1,0:T(8,128)S(1)}, s32[16,512]{1,0:T(8,128)S(1)}) fusion(pred[]{:T(512)S(6)} %eq.4, s32[16,512]{1,0:T(8,128)} %param.6, s32[16,512]{1,0:T(8,128)} %param.8, s32[16,512]{1,0:T(8,128)} %param.5, s32[16,512]{1,0:T(8,128)} %param.7), kind=kLoop, calls=%fused_computation.2 | loop fusion | flops 24576 | bytes 229377 | tf_op jit(solution)/shard_map/jit(_where)/select_n | solution.py:265
  1.5 3.9 %collective-permute-start = (s32[16,512]{1,0:T(8,128)S(1)}, s32[16,512]{1,0:T(8,128)S(1)}, u32[]{:S(2)}, u32[]{:S(2)}) collective-permute-start(s32[16,512]{1,0:T(8,128)S(1)} %get-tuple-element.12), channel_id=1, source_target_pairs={{0,510},{1,3},{2,0},{3,5},{4,2},{5,7},{6,4},{7,9},{8,6},{9,11},{10... | collective-permute-start | bytes 98312 | tf_op jit(solution)/shard_map/ppermute | solution.py:264
  5.4 15.1 %all_gather.3.chip_ref = s32[64,512]{1,0:T(8,128)S(1)} all-gather(s32[32,512]{1,0:T(8,128)S(1)} %pad_add_fusion), channel_id=1, replica_groups=mesh['z'=8,'y'=8,'x'=4,'core'=2] {'core'}, dimensions={0}, use_global_device_ids=true | all-gather | bytes 196608 | tf_op jit(solution)/shard_map/all_gather | solution.py:258
  20.6 1.9 %collective-permute-start.1 = (s32[48,512]{1,0:T(8,128)S(1)}, s32[48,512]{1,0:T(8,128)S(1)}, u32[]{:S(2)}, u32[]{:S(2)}) collective-permute-start(s32[48,512]{1,0:T(8,128)S(1)} %slice_select_fusion), channel_id=1, source_target_pairs={{0,511},{1,2},{2,1},{3,4},{4,3},{5,6},{6,5},{7,8},{8,7},{9,10},{10... | collective-permute-start | bytes 294920 | tf_op jit(solution)/shard_map/ppermute | solution.py:259
  23.2 1.1 %shard_map.68.chip_ref = f8e4m3fn[9,512,512]{2,1,0:T(32,128)(4,1)S(1)} custom-call(s32[1]{0:T(128)S(6)} %sub.3.thresh_ref, s32[64,512]{1,0:T(8,128)S(1)} %all_gather.3.chip_ref), custom_call_target="tpu_custom_call" | custom-call | flops 1342177280 | tf_op jit(solution)/shard_map/pallas_call | solution.py:210
  24.3 2.2 %collective-permute-done.1.far_ref = s32[48,512]{1,0:T(8,128)S(1)} collective-permute-done((s32[48,512]{1,0:T(8,128)S(1)}, s32[48,512]{1,0:T(8,128)S(1)}, u32[]{:S(2)}, u32[]{:S(2)}) %collective-permute-start.1) | collective-permute-done | bytes 98336 | tf_op jit(solution)/shard_map/ppermute | solution.py:259
  26.5 2.8 %shard_map.69 = (f32[512,1024]{1,0:T(8,128)S(1)}, f8e4m3fn[3,512,512]{2,1,0:T(32,128)(4,1)S(1)}, f32[8,128]{1,0:T(8,128)S(1)}) custom-call(s32[1]{0:T(128)} %bitcast.core_ref, s32[1]{0:T(128)S(6)} %sub.3.thresh_ref, s32[48,512]{1,0:T(8,128)S(1)} %collective-permute-done.1.far_ref, f8e4m3fn[9,512,512]{2,1,0:T(32,128)(4,1)S(1)} %shard_map.68.chip_ref), custom_call_target="tpu_custom_call" | custom-call | flops 4831838208 | tf_op jit(solution)/shard_map/pallas_call | solution.py:221
  29.3 0.0 collective-permute-done.near_ref
  29.3 1.4 %shard_map.70 = (f32[512,1024]{1,0:T(8,128)S(1)}, s32[16,1,128]{2,1,0:T(1,128)S(1)}) custom-call(s32[1]{0:T(128)} %bitcast.core_ref, s32[1]{0:T(128)S(6)} %sub.3.thresh_ref, s32[16,512]{1,0:T(8,128)S(1)} %collective-permute-done.near_ref, f8e4m3fn[9,512,512]{2,1,0:T(32,128)(4,1)S(1)} %shard_map.68.chip_ref, ...), custom_call_target="tpu_custom_call", output_to_operand_aliasing={{0}: (6, {})} | custom-call | flops 1879048192 | tf_op jit(solution)/shard_map/pallas_call | solution.py:237
  30.7 15.7 %all_to_all.10 = s32[16,1,128]{2,1,0:T(1,128)S(1)} all-to-all(s32[16,1,128]{2,1,0:T(1,128)S(1)} %get-tuple-element.11), channel_id=1, replica_groups=mesh['z'=8,'y'=8,'x'=4,'core'=2] {'y','core'}, dimensions={0} | all-to-all | bytes 16384 | tf_op jit(solution)/shard_map/all_to_all | solution.py:273
  46.4 0.6 %broadcast_in_dim.2 = s32[32,1,128]{2,1,0:T(1,128)} broadcast(s32[128]{0:T(128)S(1)} %reduce_sum.18), dimensions={2} | broadcast | bytes 16896 | tf_op jit(solution)/shard_map/broadcast_in_dim | solution.py:274
  47.1 3.8 %all-to-all-start.1 = ((s32[32,1,128]{2,1,0:T(1,128)}), s32[32,1,128]{2,1,0:T(1,128)S(1)}, u32[]{:S(2)}, u32[]{:S(2)}) async-start(s32[32,1,128]{2,1,0:T(1,128)} %broadcast_in_dim.2), calls=%async_computation.1 | async-start | bytes 32768 | tf_op jit(solution)/shard_map/all_to_all | solution.py:275
  50.9 1.3 %copy.10 = f32[512,1024]{1,0:T(8,128)} copy(f32[512,1024]{1,0:T(8,128)S(1)} %get-tuple-element.15) | data formatting | bytes 4194304
  52.2 7.1 %all-to-all-done.1 = s32[32,1,128]{2,1,0:T(1,128)S(1)} async-done(((s32[32,1,128]{2,1,0:T(1,128)}), s32[32,1,128]{2,1,0:T(1,128)S(1)}, u32[]{:S(2)}, u32[]{:S(2)}) %all-to-all-start.1) | async-done | bytes 16416 | tf_op jit(solution)/shard_map/all_to_all | solution.py:275
  59.3 0.5 reduce_sum.19
  (3 shorter events, 0.1 us)
Async XLA Ops:
  1.5 27.8 %collective-permute-start = (s32[16,512]{1,0:T(8,128)S(1)}, s32[16,512]{1,0:T(8,128)S(1)}, u32[]{:S(2)}, u32[]{:S(2)}) collective-permute-start(s32[16,512]{1,0:T(8,128)S(1)} %get-tuple-element.12), channel_id=1, source_target_pairs={{0,510},{1,3},{2,0},{3,5},{4,2},{5,7},{6,4},{7,9},{8,6},{9,11},{10... | collective-permute-start | bytes 98312 | tf_op jit(solution)/shard_map/ppermute | solution.py:264
  20.6 5.9 %collective-permute-start.1 = (s32[48,512]{1,0:T(8,128)S(1)}, s32[48,512]{1,0:T(8,128)S(1)}, u32[]{:S(2)}, u32[]{:S(2)}) collective-permute-start(s32[48,512]{1,0:T(8,128)S(1)} %slice_select_fusion), channel_id=1, source_target_pairs={{0,511},{1,2},{2,1},{3,4},{4,3},{5,6},{6,5},{7,8},{8,7},{9,10},{10... | collective-permute-start | bytes 294920 | tf_op jit(solution)/shard_map/ppermute | solution.py:259
  47.1 12.3 %all-to-all-start.1 = ((s32[32,1,128]{2,1,0:T(1,128)}), s32[32,1,128]{2,1,0:T(1,128)S(1)}, u32[]{:S(2)}, u32[]{:S(2)}) async-start(s32[32,1,128]{2,1,0:T(1,128)} %broadcast_in_dim.2), calls=%async_computation.1 | async-start | bytes 32768 | tf_op jit(solution)/shard_map/all_to_all | solution.py:275

commit v4 on v3

--- a/solution.py
+++ b/solution.py
@@ -1,7 +1,9 @@
 import functools
+import math
 
 import jax
 import jax.numpy as jnp
+import numpy as np
 from jax import lax
 from jax.experimental import pallas as pl
 from jax.experimental.pallas import tpu as pltpu
@@ -15,8 +17,8 @@
 WORDS = TILE // 32
 SIDE = 128
 ROWS = ("z", "y", "x", "core")
-FIRST = ("y", "core")
-SECOND = ("z", "x")
+SIZES = (8, 8, 4, 2)
+MIDDLE = (6, 6, 2, 1)
 KIND = jnp.float8_e4m3fn
 WIDE = jnp.bfloat16
 MIB = 1024 * 1024
@@ -249,6 +251,20 @@
     )(core, thresh, near, tiles, mids, sums, support)
 
 
+def exchange_groups(axes):
+    ids = np.arange(math.prod(SIZES)).reshape(SIZES)
+    ids = np.roll(ids, [-at for at in MIDDLE], axis=range(4))
+    kept = [axis for axis in range(4) if axis not in axes]
+    members = math.prod(SIZES[axis] for axis in axes)
+    return ids.transpose(kept + list(axes)).reshape(-1, members).tolist()
+
+
+def exchange(values, axes):
+    groups = exchange_groups(axes)
+    values = jnp.broadcast_to(values, (len(groups[0]), 1, 128))
+    return lax.all_to_all(values, ROWS, 0, 0, axis_index_groups=groups)
+
+
 def on_device(adj_diag, adj_right, alive_diag, alive_right, truss_k):
     count = lax.axis_size(ROWS)
     core = lax.axis_index("core")
@@ -270,9 +286,8 @@
     tiles = chip_tiles(thresh, chip)
     support, mids, sums = main_part(core, thresh, far, tiles)
     support, removed = edge_part(core, thresh, near, tiles, mids, sums, support)
-    removed = jnp.sum(lax.all_to_all(removed, FIRST, 0, 0), axis=0, keepdims=True)
-    removed = jnp.broadcast_to(removed, (32, 1, 128))
-    removed = jnp.sum(lax.all_to_all(removed, SECOND, 0, 0), axis=(0, 1))
+    removed = jnp.sum(exchange(removed, (1, 3)), axis=0, keepdims=True)
+    removed = jnp.sum(exchange(removed, (0, 2)), axis=(0, 1))
     return (support, removed[:ITERS])
 
 

time: 60.2 us -> 58.1 us (0.965)
  waiting for transfers between devices: 9.35 us -> 4.17 us
  starting transfers between devices: 9.66 us -> 13.3 us
  blocking collectives: 30.9 us -> 29.8 us
    all_to_all x1, waiting for transfers between devices: 7.13 us -> 1.96 us  [exchange(): return lax.all_to_all(values, ROWS, 0, 0, axis_index_groups=groups)]
    all_to_all x1, starting transfers between devices: 3.8 us -> 7.41 us  [exchange(): return lax.all_to_all(values, ROWS, 0, 0, axis_index_groups=groups)]
    all_to_all x1, blocking collectives: 15.7 us -> 14.7 us  [exchange(): return lax.all_to_all(values, ROWS, 0, 0, axis_index_groups=groups)]
where the time goes in v4:
time: 58.1 us; the launch traced here: 57.2 us
  blocking collectives  29.8 us (51%)
  starting transfers between devices  13.3 us (23%)
  Pallas kernels  5.29 us (9%)
  waiting for transfers between devices  4.17 us (7%)
  local copies, waits for them, and re-layouts  1.93 us (3%)
  other arithmetic  1.4 us (2%)
  between operations  1.35 us (2%)
    all_gather x1, blocking collectives, on_device(): lax.all_gather(jnp.concatenate([within, across], axis=0), 'core', tiled=T...  15.1 us
    all_to_all x1, blocking collectives, exchange(): return lax.all_to_all(values, ROWS, 0, 0, axis_index_groups=groups)  14.7 us
    all_to_all x1, starting transfers between devices, exchange(): return lax.all_to_all(values, ROWS, 0, 0, axis_index_groups=groups)  7.41 us
    ppermute x1, starting transfers between devices, on_device(): lax.ppermute(jnp.where(core == 0, within, across), ROWS, [(i, (i + 2 if i...  3.94 us
    pallas_call x1, Pallas kernels, main_part(): pl.pallas_call(main_kernel, out_shape=(pltpu.VMEM((TILE, 2 * TILE), jnp.f...  2.77 us
    ppermute x1, waiting for transfers between devices, on_device(): lax.ppermute(jnp.where(core == 0, chip[:3 * WORDS], chip[WORDS:]), ROWS,...  2.21 us
    all_to_all x1, waiting for transfers between devices, exchange(): return lax.all_to_all(values, ROWS, 0, 0, axis_index_groups=groups)  1.96 us
    ppermute x1, starting transfers between devices, on_device(): lax.ppermute(jnp.where(core == 0, chip[:3 * WORDS], chip[WORDS:]), ROWS,...  1.92 us
  transfers between devices with their start and end apart: 3, of which 2 were waited for; matrix products, arithmetic and copies ran while one was open for 2% of the time, Pallas kernels for 7%

profile of v4, /device:TPU:1, one launch (start us, length us, event | category | flops | bytes accessed | tf_op | source)
XLA Modules:
  0.0 57.2 jit_solution(17277270069075242009)
XLA Ops:
  0.6 0.8 %broadcast_select_fusion = (s32[16,512]{1,0:T(8,128)S(1)}, s32[16,512]{1,0:T(8,128)S(1)}, s32[16,512]{1,0:T(8,128)S(1)}) fusion(pred[]{:T(512)S(6)} %eq.4, s32[16,512]{1,0:T(8,128)} %param.6, s32[16,512]{1,0:T(8,128)} %param.8, s32[16,512]{1,0:T(8,128)} %param.5, s32[16,512]{1,0:T(8,128)} %param.7), kind=kLoop, calls=%fused_computation.2 | loop fusion | flops 24576 | bytes 229377 | tf_op jit(solution)/shard_map/jit(_where)/select_n | solution.py:281
  1.5 3.9 %collective-permute-start = (s32[16,512]{1,0:T(8,128)S(1)}, s32[16,512]{1,0:T(8,128)S(1)}, u32[]{:S(2)}, u32[]{:S(2)}) collective-permute-start(s32[16,512]{1,0:T(8,128)S(1)} %get-tuple-element.12), channel_id=1, source_target_pairs={{0,510},{1,3},{2,0},{3,5},{4,2},{5,7},{6,4},{7,9},{8,6},{9,11},{10... | collective-permute-start | bytes 98312 | tf_op jit(solution)/shard_map/ppermute | solution.py:280
  5.4 15.1 %all_gather.3.chip_ref = s32[64,512]{1,0:T(8,128)S(1)} all-gather(s32[32,512]{1,0:T(8,128)S(1)} %pad_add_fusion), channel_id=1, replica_groups=mesh['z'=8,'y'=8,'x'=4,'core'=2] {'core'}, dimensions={0}, use_global_device_ids=true | all-gather | bytes 196608 | tf_op jit(solution)/shard_map/all_gather | solution.py:274
  20.6 1.9 %collective-permute-start.1 = (s32[48,512]{1,0:T(8,128)S(1)}, s32[48,512]{1,0:T(8,128)S(1)}, u32[]{:S(2)}, u32[]{:S(2)}) collective-permute-start(s32[48,512]{1,0:T(8,128)S(1)} %slice_select_fusion), channel_id=1, source_target_pairs={{0,511},{1,2},{2,1},{3,4},{4,3},{5,6},{6,5},{7,8},{8,7},{9,10},{10... | collective-permute-start | bytes 294920 | tf_op jit(solution)/shard_map/ppermute | solution.py:275
  23.2 1.1 %shard_map.68.chip_ref = f8e4m3fn[9,512,512]{2,1,0:T(32,128)(4,1)S(1)} custom-call(s32[1]{0:T(128)S(6)} %sub.3.thresh_ref, s32[64,512]{1,0:T(8,128)S(1)} %all_gather.3.chip_ref), custom_call_target="tpu_custom_call" | custom-call | flops 1342177280 | tf_op jit(solution)/shard_map/pallas_call | solution.py:212
  24.3 2.2 %collective-permute-done.1.far_ref = s32[48,512]{1,0:T(8,128)S(1)} collective-permute-done((s32[48,512]{1,0:T(8,128)S(1)}, s32[48,512]{1,0:T(8,128)S(1)}, u32[]{:S(2)}, u32[]{:S(2)}) %collective-permute-start.1) | collective-permute-done | bytes 98336 | tf_op jit(solution)/shard_map/ppermute | solution.py:275
  26.5 2.8 %shard_map.69 = (f32[512,1024]{1,0:T(8,128)S(1)}, f8e4m3fn[3,512,512]{2,1,0:T(32,128)(4,1)S(1)}, f32[8,128]{1,0:T(8,128)S(1)}) custom-call(s32[1]{0:T(128)} %bitcast.core_ref, s32[1]{0:T(128)S(6)} %sub.3.thresh_ref, s32[48,512]{1,0:T(8,128)S(1)} %collective-permute-done.1.far_ref, f8e4m3fn[9,512,512]{2,1,0:T(32,128)(4,1)S(1)} %shard_map.68.chip_ref), custom_call_target="tpu_custom_call" | custom-call | flops 4831838208 | tf_op jit(solution)/shard_map/pallas_call | solution.py:223
  29.3 0.0 collective-permute-done.near_ref
  29.3 1.4 %shard_map.70 = (f32[512,1024]{1,0:T(8,128)S(1)}, s32[16,1,128]{2,1,0:T(1,128)S(1)}) custom-call(s32[1]{0:T(128)} %bitcast.core_ref, s32[1]{0:T(128)S(6)} %sub.3.thresh_ref, s32[16,512]{1,0:T(8,128)S(1)} %collective-permute-done.near_ref, f8e4m3fn[9,512,512]{2,1,0:T(32,128)(4,1)S(1)} %shard_map.68.chip_ref, ...), custom_call_target="tpu_custom_call", output_to_operand_aliasing={{0}: (6, {})} | custom-call | flops 1879048192 | tf_op jit(solution)/shard_map/pallas_call | solution.py:239
  30.7 14.7 %all_to_all.10 = s32[16,1,128]{2,1,0:T(1,128)S(1)} all-to-all(s32[16,1,128]{2,1,0:T(1,128)S(1)} %get-tuple-element.11), channel_id=1, replica_groups={{437,436,445,444,389,388,397,396,405,404,413,412,421,420,429,428},{439,..., dimensions={0} | all-to-all | bytes 16384 | tf_op jit(solution)/shard_map/all_to_all | solution.py:265
  45.4 0.6 %broadcast_in_dim.2 = s32[32,1,128]{2,1,0:T(1,128)} broadcast(s32[128]{0:T(128)S(1)} %reduce_sum.18), dimensions={2} | broadcast | bytes 16896 | tf_op jit(solution)/shard_map/broadcast_in_dim | solution.py:264
  46.0 7.4 %all-to-all-start.1 = ((s32[32,1,128]{2,1,0:T(1,128)}), s32[32,1,128]{2,1,0:T(1,128)S(1)}, u32[]{:S(2)}, u32[]{:S(2)}) async-start(s32[32,1,128]{2,1,0:T(1,128)} %broadcast_in_dim.2), calls=%async_computation.1 | async-start | bytes 32768 | tf_op jit(solution)/shard_map/all_to_all | solution.py:265
  53.4 1.3 %copy.10 = f32[512,1024]{1,0:T(8,128)} copy(f32[512,1024]{1,0:T(8,128)S(1)} %get-tuple-element.15) | data formatting | bytes 4194304
  54.8 2.0 %all-to-all-done.1 = s32[32,1,128]{2,1,0:T(1,128)S(1)} async-done(((s32[32,1,128]{2,1,0:T(1,128)}), s32[32,1,128]{2,1,0:T(1,128)S(1)}, u32[]{:S(2)}, u32[]{:S(2)}) %all-to-all-start.1) | async-done | bytes 16416 | tf_op jit(solution)/shard_map/all_to_all | solution.py:265
  56.7 0.5 reduce_sum.19
  (3 shorter events, 0.1 us)
Async XLA Ops:
  1.5 27.8 %collective-permute-start = (s32[16,512]{1,0:T(8,128)S(1)}, s32[16,512]{1,0:T(8,128)S(1)}, u32[]{:S(2)}, u32[]{:S(2)}) collective-permute-start(s32[16,512]{1,0:T(8,128)S(1)} %get-tuple-element.12), channel_id=1, source_target_pairs={{0,510},{1,3},{2,0},{3,5},{4,2},{5,7},{6,4},{7,9},{8,6},{9,11},{10... | collective-permute-start | bytes 98312 | tf_op jit(solution)/shard_map/ppermute | solution.py:280
  20.6 5.9 %collective-permute-start.1 = (s32[48,512]{1,0:T(8,128)S(1)}, s32[48,512]{1,0:T(8,128)S(1)}, u32[]{:S(2)}, u32[]{:S(2)}) collective-permute-start(s32[48,512]{1,0:T(8,128)S(1)} %slice_select_fusion), channel_id=1, source_target_pairs={{0,511},{1,2},{2,1},{3,4},{4,3},{5,6},{6,5},{7,8},{8,7},{9,10},{10... | collective-permute-start | bytes 294920 | tf_op jit(solution)/shard_map/ppermute | solution.py:275
  46.0 10.7 %all-to-all-start.1 = ((s32[32,1,128]{2,1,0:T(1,128)}), s32[32,1,128]{2,1,0:T(1,128)S(1)}, u32[]{:S(2)}, u32[]{:S(2)}) async-start(s32[32,1,128]{2,1,0:T(1,128)} %broadcast_in_dim.2), calls=%async_computation.1 | async-start | bytes 32768 | tf_op jit(solution)/shard_map/all_to_all | solution.py:265
